TPU v7x, 32 devices: a whole 2x2x4 slice. The times are simulated.
32 devices in a mesh: dom: 32 (over z, y, x, core).
Axes of the slice: x: 2, y: 2, z: 4, core: 2. Of those that a mesh axis runs over, the one named last changes fastest.
Arguments:
- particles: bfloat16 [1024, 2, 7488], P('dom'), may hold values from -6 to 6
- references: bfloat16 [32, 2, 7488], P('dom'), may hold values from -6 to 6
- assignment: int32 [1024, 1], P('dom'), may hold values from 0 to 31
- orientation: int32 [1024], P('dom'), may hold values from 0 to 35
- tilt_range: int32 [2, 1024], P(None, 'dom'), may hold values from 0 to 20
Outputs:
- scores: float32 [1024, 32], P('dom')
- class_means: float32 [32, 2, 7488], P('dom')
- class_load: float32 [32], replicated
Inputs may be any that keep to these rules, and one draw needn't show every extreme that they name: `assignment`: every class has at least one particle.
All inputs are finite; a program needn't handle non-finite values.
Results may differ from a plain program's by a relative error of at most 0.0035.
Values may be sent and summed in bfloat16 or wider, within the bound.
A program may use at most 128 MiB of HBM per device.

v0:
```python
import functools
import math

import jax
import jax.numpy as jnp
from jax import lax
from jax.experimental import pallas as pl
from jax.experimental.pallas import tpu as pltpu
from jax.sharding import PartitionSpec as P

GRID = 24
ORIENTS = 36
EPS = 1e-06
GAIN = 6.0
TAU = 0.5
LANES = 128
MESH = pl.DeviceIdType.MESH


def factor(devices):
    chips = devices // 2
    inner = 1
    while inner * inner < chips:
        inner *= 2
    return chips // inner, inner


CHUNKS = 3
SUB = 640


def column(row):
    rows = row.shape[1]
    line = lax.broadcasted_iota(jnp.int32, (rows, rows), 0)
    lane = lax.broadcasted_iota(jnp.int32, (rows, rows), 1)
    return jnp.sum(jnp.where(line == lane, row, 0.0), axis=1, keepdims=True)


def frequencies(first, width):
    index = (lax.broadcasted_iota(jnp.int32, (1, width), 1) + first).astype(jnp.float32)
    plane = jnp.floor((index + 0.5) * (1.0 / (GRID * GRID)))
    rest = index - plane * (GRID * GRID)
    col_x = jnp.floor((rest + 0.5) * (1.0 / GRID))
    col_z = rest - col_x * GRID
    freq_x = jnp.where(col_x >= GRID // 2, col_x - GRID, col_x)
    freq_z = jnp.where(col_z >= GRID // 2, col_z - GRID, col_z)
    return freq_x, plane, freq_z, index


def kernel(
    outer, inner, span, coef, total,
    part_ref, ref_ref, cls_ref, orient_ref, tilt_ref,
    scores_ref, means_ref, load_ref,
    data, low, all_ref, mine, send_core, recv_core, send_in, recv_in, send_out, recv_out,
    small_send, small_recv,
    ag_send_out, ag_send_in, ag_send_core, ag_recv,
    core_send_sems, core_recv_sems, in_send_sems, in_recv_sems, out_send_sems, out_recv_sems,
    small_send_sems, small_recv_sems, local_sem,
):
    me = lax.axis_index("dom")
    core = lax.rem(me, 2)
    chip = me // 2
    b = lax.rem(chip, inner)
    a = chip // inner
    sibling = me + 1 - 2 * core
    classes = 2 * outer * inner
    half = classes // 2
    rows = part_ref.shape[0]

    def device(a_at, b_at, c_at):
        return (a_at * inner + b_at) * 2 + c_at

    def in_peer(j):
        return device(a, lax.rem(b + j, inner), core)

    def out_peer(i):
        return device(lax.rem(a + i, outer), b, core)

    barrier = pltpu.get_barrier_semaphore()
    pl.semaphore_signal(barrier, inc=1, device_id=(sibling,), device_id_type=MESH)
    for j in range(1, inner):
        pl.semaphore_signal(barrier, inc=1, device_id=(in_peer(j),), device_id_type=MESH)
    for i in range(1, outer):
        pl.semaphore_signal(barrier, inc=1, device_id=(out_peer(i),), device_id_type=MESH)
    local = pltpu.make_async_copy(ref_ref.at[0], all_ref.at[me], local_sem)
    local.start()

    def push(src, dst, send_sem, recv_sem, target):
        copy = pltpu.make_async_remote_copy(
            src_ref=src, dst_ref=dst, send_sem=send_sem, recv_sem=recv_sem,
            device_id=(target,), device_id_type=MESH,
        )
        copy.start()
        return copy

    pending = []

    def arrived(place):
        pltpu.make_async_remote_copy(
            src_ref=all_ref.at[place], dst_ref=all_ref.at[place],
            send_sem=local_sem, recv_sem=ag_recv.at[place],
            device_id=(sibling,), device_id_type=MESH,
        ).wait_recv()

    angle = orient_ref[...].astype(jnp.float32) * (2.0 * math.pi / ORIENTS)
    bins = tilt_ref[...].astype(jnp.float32)
    low_end = -(40.0 + 1.5 * bins[0:1]) * (math.pi / 180.0)
    high_end = (40.0 + 1.5 * bins[1:2]) * (math.pi / 180.0)
    sin_a, cos_a = column(jnp.sin(angle)), column(jnp.cos(angle))
    cos_c = column(jnp.cos(low_end + high_end))
    sin_c = column(jnp.sin(low_end + high_end))
    cos_w = column(jnp.cos(high_end - low_end))
    cls_row = cls_ref[...].astype(jnp.float32)
    cls_col = column(cls_row)

    row = lax.broadcasted_iota(jnp.int32, (classes, 1), 0)
    log_outer = outer.bit_length() - 1
    log_half = half.bit_length() - 1
    row_i = row & (outer - 1)
    row_j = lax.shift_right_logical(row, log_outer) & (inner - 1)
    row_c = lax.shift_right_logical(row, log_half)
    ids = (((row_i + a) & (outer - 1)) * inner + ((row_j + b) & (inner - 1))) * 2 + ((row_c + core) & 1)
    onehot = jnp.where(ids.astype(jnp.float32) == cls_row, 1.0, 0.0).astype(jnp.bfloat16)

    wedge_sum = jnp.zeros((rows, 1), jnp.float32)
    power = jnp.zeros((rows, 1), jnp.float32)
    core_copies = []
    in_copies = [[] for _ in range(CHUNKS)]
    out_copies = [[] for _ in range(CHUNKS)]

    def inner_sends(t):
        core_copies[t].wait_recv()
        for j in range(1, inner):
            lines = slice(j * outer, (j + 1) * outer)
            send_in[t, j - 1] = (mine[t, lines] + recv_core[t, lines].astype(jnp.float32)).astype(jnp.bfloat16)
            in_copies[t].append(push(
                send_in.at[t, j - 1], recv_in.at[t, j - 1],
                in_send_sems.at[t, j - 1], in_recv_sems.at[t, j - 1], in_peer(j)))
        mine[t, :outer] = mine[t, :outer] + recv_core[t, :outer].astype(jnp.float32)

    def outer_sends(t):
        for copy in in_copies[t]:
            copy.wait_recv()
        piece = mine[t, :outer]
        for j in range(1, inner):
            piece = piece + recv_in[t, j - 1].astype(jnp.float32)
        wide = 3 * span // 2
        for i in range(1, outer):
            send_out[t, i - 1] = jnp.concatenate(
                [piece[i:i + 1, :wide], piece[i:i + 1, wide:]], axis=0).astype(jnp.bfloat16)
            out_copies[t].append(push(
                send_out.at[t, i - 1], recv_out.at[t, i - 1],
                out_send_sems.at[t, i - 1], out_recv_sems.at[t, i - 1], out_peer(i)))
        return jnp.concatenate([piece[0:1, :wide], piece[0:1, wide:]], axis=0)

    def parts(first):
        width = max(0, min(SUB, coef - first))
        pieces = []
        if width:
            both = part_ref[:, :, first:first + width].astype(jnp.float32)
            pieces.append(jnp.swapaxes(both, 0, 1))
        if width < SUB:
            pieces.append(jnp.zeros((2, rows, SUB - width), jnp.float32))
        both = jnp.concatenate(pieces, axis=2) if len(pieces) > 1 else pieces[0]
        return both[0], both[1]

    for t in range(CHUNKS):
        for s in range(span // SUB):
            first = t * span + s * SUB
            freq_x, freq_y, freq_z, index = frequencies(first, SUB)
            along = freq_y * cos_a - freq_x * sin_a
            along_sq = along * along
            z_sq = freq_z * freq_z
            scale = 1.0 / (along_sq + (z_sq + 1.0))
            value = ((along_sq - z_sq) * cos_c - (2.0 * along * freq_z) * sin_c) * scale - cos_w
            wedge = 1.0 / (1.0 + jnp.exp(value * (-GAIN)))
            real, imag = parts(first)
            power = power + jnp.sum(wedge * (real * real + imag * imag), axis=1, keepdims=True)
            inside = wedge if first + SUB <= coef else jnp.where(index < coef, wedge, 0.0)
            wedge_sum = wedge_sum + jnp.sum(inside, axis=1, keepdims=True)
            at = s * SUB
            data[t, :, at:at + SUB] = (wedge * real).astype(jnp.bfloat16)
            data[t, :, span + at:span + at + SUB] = (wedge * imag).astype(jnp.bfloat16)
            data[t, :, 2 * span + at:2 * span + at + SUB] = (wedge * wedge).astype(jnp.bfloat16)
            low[:, first:first + SUB] = wedge.astype(jnp.bfloat16)
        for q in range(3):
            cols = slice(q * span, (q + 1) * span)
            sums = jnp.dot(onehot, data[t, :, cols], preferred_element_type=jnp.float32)
            send_core[t, :, cols] = sums[half:].astype(jnp.bfloat16)
            mine[t, :, cols] = sums[:half]
        if t == 0:
            pl.semaphore_wait(barrier, 1 + (inner - 1) + (outer - 1))
            for i in range(1, outer):
                pending.append(push(ref_ref.at[0], all_ref.at[me], ag_send_out.at[i - 1], ag_recv.at[me], out_peer(i)))
            for j in range(1, inner):
                pending.append(push(ref_ref.at[0], all_ref.at[me], ag_send_in.at[0, j - 1], ag_recv.at[me], in_peer(j)))
        core_copies.append(push(send_core.at[t], recv_core.at[t], core_send_sems.at[t], core_recv_sems.at[t], sibling))
        if t == 0:
            pending.append(push(ref_ref.at[0], all_ref.at[me], ag_send_core.at[0], ag_recv.at[me], sibling))
        else:
            inner_sends(t - 1)
        if t == CHUNKS - 1:
            wide = small_send.shape[2] // 2
            lane = lax.broadcasted_iota(jnp.int32, (rows, wide), 1).astype(jnp.float32)
            hits = jnp.where(lane == cls_col, 1.0, 0.0)
            small_send[0, :, :wide] = jnp.sum(hits, axis=0, keepdims=True)
            small_send[0, :, wide:] = jnp.sum(hits * wedge_sum, axis=0, keepdims=True)
    small = [push(small_send.at[0], small_recv.at[0], small_send_sems.at[0], small_recv_sems.at[0], sibling)]
    inner_sends(CHUNKS - 1)
    small[0].wait_recv()
    small_send[1] = small_send[0] + small_recv[0]

    for j in range(1, inner):
        small.append(push(small_send.at[1], small_recv.at[j], small_send_sems.at[j], small_recv_sems.at[j], in_peer(j)))

    for i in range(1, outer):
        place = device(lax.rem(a + outer - i, outer), b, core)
        arrived(place)
        for j in range(1, inner):
            pending.append(push(all_ref.at[place], all_ref.at[place], ag_send_in.at[i, j - 1], ag_recv.at[place], in_peer(j)))
        pending.append(push(all_ref.at[place], all_ref.at[place], ag_send_core.at[i], ag_recv.at[place], sibling))

    own = [outer_sends(t) for t in range(CHUNKS)]
    tally = small_send[1]
    for j in range(1, inner):
        small[j].wait_recv()
        tally = tally + small_recv[j]
    small_send[2] = tally

    for i in range(1, outer):
        at = inner + i - 1
        small.append(push(small_send.at[2], small_recv.at[at], small_send_sems.at[at], small_recv_sems.at[at], out_peer(i)))
    slot = outer
    for i in range(outer):
        for j in range(1, inner):
            place = device(lax.rem(a + outer - i, outer), lax.rem(b + inner - j, inner), core)
            arrived(place)
            pending.append(push(all_ref.at[place], all_ref.at[place], ag_send_core.at[slot], ag_recv.at[place], sibling))
            slot += 1

    for i in range(outer):
        for j in range(inner):
            arrived(device(lax.rem(a + i, outer), lax.rem(b + j, inner), 1 - core))
    local.wait()
    nt = (((1,), (1,)), ((), ()))
    group = min(classes, 32)
    for g in range(classes // group):
        inter = jnp.zeros((rows, group), jnp.float32)
        energy = jnp.zeros((rows, group), jnp.float32)
        lines = slice(g * group, (g + 1) * group)
        for t in range(CHUNKS):
            width = min(span, coef - t * span)
            cols = slice(t * span, t * span + width)
            both = jnp.swapaxes(all_ref[lines, :, cols].astype(jnp.float32), 0, 1)
            real, imag = both[0], both[1]
            ref_power = (real * real + imag * imag).astype(jnp.bfloat16)
            inter = inter + lax.dot_general(data[t, :, :width], real.astype(jnp.bfloat16), nt, preferred_element_type=jnp.float32)
            inter = inter + lax.dot_general(data[t, :, span:span + width], imag.astype(jnp.bfloat16), nt, preferred_element_type=jnp.float32)
            energy = energy + lax.dot_general(low[:, cols], ref_power, nt, preferred_element_type=jnp.float32)
        scores_ref[:, lines] = inter / (
            math.sqrt(coef) * jnp.sqrt((energy / coef + EPS) * (power / coef + EPS)))
    for i in range(1, outer):
        small[inner + i - 1].wait_recv()
        tally = tally + small_recv[inner + i - 1]
    wide = tally.shape[1] // 2
    load_ref[...] = tally[:, :classes] * classes / total
    lane = lax.broadcasted_iota(jnp.int32, (1, wide), 1)
    wedge_total = jnp.sum(jnp.where(lane == me, tally[:, wide:], 0.0), axis=1, keepdims=True)
    floor = TAU * (wedge_total / coef + 1.0)
    for t in range(CHUNKS):
        for copy in out_copies[t]:
            copy.wait_recv()
        whole = own[t]
        for i in range(1, outer):
            whole = whole + recv_out[t, i - 1].astype(jnp.float32)
        flat = jnp.concatenate([whole[0:1], whole[1:2]], axis=1)
        scale = 1.0 / (flat[:, 2 * span:] + floor)
        width = min(span, coef - t * span)
        for q in range(2):
            mean = flat[:, q * span:(q + 1) * span] * scale
            means_ref[0, q:q + 1, t * span:t * span + width] = mean[:, :width]

    for copy in pending + core_copies + small + sum(in_copies, []) + sum(out_copies, []):
        copy.wait_send()


def finish(*arrays):
    def put(*refs):
        for src, dst in zip(refs[:len(arrays)], refs[len(arrays):]):
            dst[...] = src[...]

    vmem = pl.BlockSpec(memory_space=pltpu.VMEM)
    scores, means, load = pl.pallas_call(
        put,
        out_shape=tuple(jax.ShapeDtypeStruct(x.shape, x.dtype) for x in arrays),
        in_specs=[vmem] * len(arrays),
        out_specs=(vmem,) * len(arrays),
    )(*arrays)
    return (scores, means, load[0])


def body(particles, references, assignment, orientation, tilt_range):
    part_rows = particles.shape[0]
    coef = particles.shape[2]
    devices = lax.axis_size("dom")
    classes = references.shape[0] * devices
    assert references.shape[0] == 1
    outer, inner = factor(devices)
    total = part_rows * devices
    unit = math.lcm(2 * LANES, SUB)
    span = -(-coef // (CHUNKS * unit)) * unit
    padded = CHUNKS * span
    width = 2 * (-(-classes // LANES) * LANES)

    vmem = pl.BlockSpec(memory_space=pltpu.VMEM)
    dma = pltpu.SemaphoreType.DMA
    bf16, f32 = jnp.bfloat16, jnp.float32
    wide = 3 * span
    scores, means, load = pl.pallas_call(
        functools.partial(kernel, outer, inner, span, coef, total),
        out_shape=(
            jax.ShapeDtypeStruct((part_rows, classes), f32),
            jax.ShapeDtypeStruct((1, 2, coef), f32),
            jax.ShapeDtypeStruct((1, classes), f32),
        ),
        in_specs=[vmem] * 5,
        out_specs=(vmem, vmem, vmem),
        scratch_shapes=[
            pltpu.VMEM((CHUNKS, part_rows, wide), bf16),
            pltpu.VMEM((part_rows, padded), bf16),
            pltpu.VMEM((classes, 2, coef), bf16),
            pltpu.VMEM((CHUNKS, classes // 2, wide), f32),
            pltpu.VMEM((CHUNKS, classes // 2, wide), bf16),
            pltpu.VMEM((CHUNKS, classes // 2, wide), bf16),
            pltpu.VMEM((CHUNKS, inner - 1, outer, wide), bf16),
            pltpu.VMEM((CHUNKS, inner - 1, outer, wide), bf16),
            pltpu.VMEM((CHUNKS, outer - 1, 2, wide // 2), bf16),
            pltpu.VMEM((CHUNKS, outer - 1, 2, wide // 2), bf16),
            pltpu.VMEM((3, 1, width), f32),
            pltpu.VMEM((inner + outer - 1, 1, width), f32),
            dma((outer,)), dma((outer, inner)), dma((outer * inner,)), dma((classes,)),
            dma((CHUNKS,)), dma((CHUNKS,)),
            dma((CHUNKS, inner)), dma((CHUNKS, inner)), dma((CHUNKS, outer)), dma((CHUNKS, outer)),
            dma((inner + outer,)), dma((inner + outer,)), dma,
        ],
        compiler_params=pltpu.CompilerParams(
            collective_id=0, has_side_effects=True, vmem_limit_bytes=60 * 1024 * 1024
        ),
    )(particles, references, assignment.reshape(1, part_rows), orientation[None, :], tilt_range)
    return finish(scores, means, load)


def solution(mesh):
    in_specs = (
        P("dom", None, None),
        P("dom", None, None),
        P("dom", None),
        P("dom"),
        P(None, "dom"),
    )
    out_specs = (P("dom", None), P("dom", None, None), P())
    return jax.shard_map(body, mesh=mesh, in_specs=in_specs, out_specs=out_specs, check_vma=False)
```

profile of v0, /device:TPU:0, one launch (start us, length us, event | category | flops | bytes accessed | tf_op | source)
XLA Modules:
  0.0 28.5 jit_solution(9527285882644175699)
XLA Ops:
  0.6 26.4 %shard_map.76 = (f32[32,32]{1,0:T(8,128)}, f32[1,2,7488]{2,1,0:T(2,128)}, f32[1,32]{1,0:T(1,128)}) custom-call(bf16[32,2,7488]{2,1,0:T(2,128)(2,1)} %part_ref.1, bf16[1,2,7488]{2,1,0:T(2,128)(2,1)} %ref_ref.1, s32[1,32]{1,0:T(1,128)} %bitcast.3, s32[1,32]{1,0:T(1,128)} %bitcast.4, s32[2,32]{1,0:T(2,128)} %tilt_ref.1), custom_call_target="tpu_custom_call" | custom-call | tf_op jit(solution)/shard_map/pallas_call | solution.py:319
  27.0 1.5 %shard_map.77 = (f32[32,32]{1,0:T(8,128)}, f32[1,2,7488]{2,1,0:T(2,128)}, f32[1,32]{1,0:T(1,128)}) custom-call(f32[32,32]{1,0:T(8,128)} %get-tuple-element.9.refs_0_, f32[1,2,7488]{2,1,0:T(2,128)} %get-tuple-element.10.refs_1_, f32[1,32]{1,0:T(1,128)} %get-tuple-element.11.refs_2_), custom_call_target="tpu_custom_call" | custom-call | tf_op jit(solution)/shard_map/pallas_call | solution.py:293
where the time goes:
time: 28.7 us; the launch traced here: 28.5 us
  Pallas kernels  27.9 us (97%)
  between operations  0.64 us (2%)
    pallas_call x1, Pallas kernels, body(): pl.pallas_call(functools.partial(kernel, outer, inner, span, coef, total)...  26.4 us
    pallas_call x1, Pallas kernels, finish(): pl.pallas_call(put, out_shape=tuple((jax.ShapeDtypeStruct(x.shape, x.dtyp...  1.46 us

commit v1 on v0

v1 whole, which is shorter than its diff:
```python
import functools
import math

import jax
import jax.numpy as jnp
from jax import lax
from jax.experimental import pallas as pl
from jax.experimental.pallas import tpu as pltpu
from jax.sharding import PartitionSpec as P

GRID = 24
ORIENTS = 36
EPS = 1e-06
GAIN = 6.0
TAU = 0.5
LANES = 128
MESH = pl.DeviceIdType.MESH

PAIRS = 3
CHUNKS = 2 * PAIRS
SUB = 640


def factor(devices):
    chips = devices // 2
    log = chips.bit_length() - 1
    gx = 1 << (log // 3)
    gy = 1 << ((log - log // 3) // 2)
    return gx, gy, chips // (gx * gy)


def column(row):
    rows = row.shape[1]
    line = lax.broadcasted_iota(jnp.int32, (rows, rows), 0)
    lane = lax.broadcasted_iota(jnp.int32, (rows, rows), 1)
    return jnp.sum(jnp.where(line == lane, row, 0.0), axis=1, keepdims=True)


def frequencies(first, width):
    index = (lax.broadcasted_iota(jnp.int32, (1, width), 1) + first).astype(jnp.float32)
    plane = jnp.floor((index + 0.5) * (1.0 / (GRID * GRID)))
    rest = index - plane * (GRID * GRID)
    col_x = jnp.floor((rest + 0.5) * (1.0 / GRID))
    col_z = rest - col_x * GRID
    freq_x = jnp.where(col_x >= GRID // 2, col_x - GRID, col_x)
    freq_z = jnp.where(col_z >= GRID // 2, col_z - GRID, col_z)
    return freq_x, plane, freq_z, index


def kernel(
    gx, gy, gz, span, coef, total,
    part_hbm, ref_hbm, cls_hbm, orient_hbm, tilt_hbm,
    scores_ref, means_ref, load_ref,
    part, cls_ref, orient_ref, tilt_ref,
    data, low, all_ref, mine, send_core, recv_core,
    s1x, r1x, s1y, r1y, s2x, r2x, s2y, r2y, s3, r3, small_send, small_recv,
    in_sems, ag_sems, ag_send_sem, core_sems, sems1, sems2, sems3, small_sems, send_sems,
):
    me = lax.axis_index("dom")
    core = lax.rem(me, 2)
    chip = me // 2
    x = lax.rem(chip, gx)
    y = lax.rem(chip // gx, gy)
    z = chip // (gx * gy)
    sibling = me + 1 - 2 * core
    classes = 2 * gx * gy * gz
    half = classes // 2
    rows = part.shape[0]
    wide = 3 * span
    cut = coef // 2 // LANES * LANES

    def device(x_at, y_at, z_at, c_at):
        return ((z_at * gy + y_at) * gx + x_at) * 2 + c_at

    def x_peer(j):
        return device(lax.rem(x + j, gx), y, z, core)

    def y_peer(j):
        return device(x, lax.rem(y + j, gy), z, core)

    def z_peer(j):
        return device(x, y, lax.rem(z + j, gz), core)

    def fetch(src, dst, at):
        copy = pltpu.make_async_copy(src, dst, in_sems.at[at])
        copy.start()
        return copy

    barrier = pltpu.get_barrier_semaphore()
    peers = [sibling]
    peers += [x_peer(j) for j in range(1, gx)]
    peers += [y_peer(j) for j in range(1, gy)]
    peers += [z_peer(j) for j in range(1, gz)]
    for peer in peers:
        pl.semaphore_signal(barrier, inc=1, device_id=(peer,), device_id_type=MESH)
    own_ref = fetch(ref_hbm.at[0], all_ref.at[0], 0)
    metas = [
        fetch(orient_hbm, orient_ref, 1),
        fetch(tilt_hbm, tilt_ref, 2),
        fetch(cls_hbm, cls_ref, 3),
    ]
    part_copies = []
    for p in range(PAIRS):
        first = 2 * p * span
        cols = pl.ds(first, min(2 * span, coef - first))
        part_copies.append(fetch(part_hbm.at[:, :, cols], part.at[:, :, cols], 4 + p))

    def push(src, dst, send_sem, recv_sem, target):
        pltpu.make_async_remote_copy(
            src_ref=src, dst_ref=dst, send_sem=send_sem, recv_sem=recv_sem,
            device_id=(target,), device_id_type=MESH,
        ).start()

    def whole_of(ref, sem):
        return pltpu.make_async_remote_copy(
            src_ref=ref, dst_ref=ref, send_sem=sem, recv_sem=sem,
            device_id=(sibling,), device_id_type=MESH,
        )

    def arrived(ref, sem):
        whole_of(ref, sem).wait_recv()

    def slot(dx, dy, dc):
        return ((dc * gx + dx) * gy + dy) * gz

    def give(src_slot, dst_slot, n, lanes, at, target):
        src = all_ref.at[pl.ds(src_slot, n), :, lanes]
        dst = all_ref.at[pl.ds(dst_slot, n), :, lanes]
        push(src, dst, ag_send_sem, ag_sems.at[at], target)

    every = slice(0, coef)
    front, back = slice(0, cut), slice(cut, coef)

    def ag_direct(at, n, sem):
        for j in range(1, gx):
            give(at, slot(gx - j, 0, 0) + at, n, every, sem, x_peer(j))
        for j in range(1, gy):
            give(at, slot(0, gy - j, 0) + at, n, every, sem + 1, y_peer(j))
        give(at, slot(0, 0, 1) + at, n, every, 0, sibling)

    def ag_forward(at, n, sem):
        if gx > 1:
            arrived(all_ref.at[pl.ds(0, (gx - 1) * n)], ag_sems.at[sem])
        for dx in range(1, gx):
            for j in range(1, gy):
                give(slot(dx, 0, 0) + at, slot(dx, gy - j, 0) + at, n, front, sem + 2, y_peer(j))
        if gy > 1:
            arrived(all_ref.at[pl.ds(0, (gy - 1) * n)], ag_sems.at[sem + 1])
        for dy in range(1, gy):
            for j in range(1, gx):
                give(slot(0, dy, 0) + at, slot(gx - j, dy, 0) + at, n, back, sem + 3, x_peer(j))
        for dx in range(1, gx):
            give(slot(dx, 0, 0) + at, slot(dx, 0, 1) + at, n, every, 0, sibling)
        for dy in range(1, gy):
            give(slot(0, dy, 0) + at, slot(0, dy, 1) + at, n, every, 0, sibling)

    def ag_core(at, n, sem):
        count = (gx - 1) * (gy - 1) * n
        if count:
            arrived(all_ref.at[pl.ds(0, count), :, front], ag_sems.at[sem + 2])
            arrived(all_ref.at[pl.ds(0, count), :, back], ag_sems.at[sem + 3])
        for dx in range(1, gx):
            for dy in range(1, gy):
                give(slot(dx, dy, 0) + at, slot(dx, dy, 1) + at, n, every, 0, sibling)

    def ag_own():
        own_ref.wait()
        for j in range(1, gz):
            give(0, gz - j, 1, every, 1, z_peer(j))
        ag_direct(0, 1, 2)

    def ag_rest():
        arrived(all_ref.at[pl.ds(1, gz - 1)], ag_sems.at[1])
        ag_direct(1, gz - 1, 6)

    for copy in metas:
        copy.wait()
    angle = orient_ref[...].astype(jnp.float32) * (2.0 * math.pi / ORIENTS)
    bins = tilt_ref[...].astype(jnp.float32)
    low_end = -(40.0 + 1.5 * bins[0:1]) * (math.pi / 180.0)
    high_end = (40.0 + 1.5 * bins[1:2]) * (math.pi / 180.0)
    sin_a, cos_a = column(jnp.sin(angle)), column(jnp.cos(angle))
    cos_c = column(jnp.cos(low_end + high_end))
    sin_c = column(jnp.sin(low_end + high_end))
    cos_w = column(jnp.cos(high_end - low_end))
    cls_row = cls_ref[...].astype(jnp.float32)
    cls_col = column(cls_row)

    def log2(n):
        return n.bit_length() - 1

    row = lax.broadcasted_iota(jnp.int32, (classes, 1), 0)
    row_z = row & (gz - 1)
    up = lax.shift_right_logical(row, log2(gz))
    row_c = lax.shift_right_logical(row, log2(half))

    def ids_of(dx, dy):
        return device((dx + x) & (gx - 1), (dy + y) & (gy - 1), (row_z + z) & (gz - 1), (row_c + core) & 1)

    ids = (
        ids_of(lax.shift_right_logical(up, log2(gy)) & (gx - 1), up & (gy - 1)),
        ids_of(up & (gx - 1), lax.shift_right_logical(up, log2(gx)) & (gy - 1)),
    )
    onehot = [jnp.where(i.astype(jnp.float32) == cls_row, 1.0, 0.0).astype(jnp.bfloat16) for i in ids]

    sizes = ((gx, gy), (gy, gx))
    hops = ((x_peer, y_peer), (y_peer, x_peer))
    one = ((s1x, r1x), (s1y, r1y))
    two = ((s2x, r2x), (s2y, r2y))
    sums = {"wedge": jnp.zeros((rows, 1), jnp.float32), "power": jnp.zeros((rows, 1), jnp.float32)}
    own = []

    def parts(first):
        width = max(0, min(SUB, coef - first))
        pieces = []
        if width:
            both = part[:, :, first:first + width].astype(jnp.float32)
            pieces.append(jnp.swapaxes(both, 0, 1))
        if width < SUB:
            pieces.append(jnp.zeros((2, rows, SUB - width), jnp.float32))
        both = jnp.concatenate(pieces, axis=2) if len(pieces) > 1 else pieces[0]
        return both[0], both[1]

    def compute(t):
        o = t % 2
        if o == 0:
            part_copies[t // 2].wait()
        for s in range(span // SUB):
            first = t * span + s * SUB
            freq_x, freq_y, freq_z, index = frequencies(first, SUB)
            along = freq_y * cos_a - freq_x * sin_a
            along_sq = along * along
            z_sq = freq_z * freq_z
            scale = 1.0 / (along_sq + (z_sq + 1.0))
            value = ((along_sq - z_sq) * cos_c - (2.0 * along * freq_z) * sin_c) * scale - cos_w
            wedge = 1.0 / (1.0 + jnp.exp(value * (-GAIN)))
            real, imag = parts(first)
            sums["power"] = sums["power"] + jnp.sum(wedge * (real * real + imag * imag), axis=1, keepdims=True)
            inside = wedge if first + SUB <= coef else jnp.where(index < coef, wedge, 0.0)
            sums["wedge"] = sums["wedge"] + jnp.sum(inside, axis=1, keepdims=True)
            at = s * SUB
            data[t, :, at:at + SUB] = (wedge * real).astype(jnp.bfloat16)
            data[t, :, span + at:span + at + SUB] = (wedge * imag).astype(jnp.bfloat16)
            data[t, :, 2 * span + at:2 * span + at + SUB] = (wedge * wedge).astype(jnp.bfloat16)
            low[:, first:first + SUB] = wedge.astype(jnp.bfloat16)
        for q in range(3):
            cols = slice(q * span, (q + 1) * span)
            both = jnp.dot(onehot[o], data[t, :, cols], preferred_element_type=jnp.float32)
            send_core[t, :, cols] = both[half:].astype(jnp.bfloat16)
            mine[t, :, cols] = both[:half]

    def cores(t):
        push(send_core.at[t], recv_core.at[t], send_sems.at[0], core_sems.at[t], sibling)

    def first(t):
        o, p = t % 2, t // 2
        send, recv = one[o]
        lines = sizes[o][1] * gz
        arrived(recv_core.at[t], core_sems.at[t])
        for j in range(1, sizes[o][0]):
            at = slice(j * lines, (j + 1) * lines)
            send[p, j - 1] = (mine[t, at] + recv_core[t, at].astype(jnp.float32)).astype(jnp.bfloat16)
            push(send.at[p, j - 1], recv.at[p, j - 1], send_sems.at[1 + o], sems1.at[t], hops[o][0](j))
        mine[t, :lines] = mine[t, :lines] + recv_core[t, :lines].astype(jnp.float32)

    def second(t):
        o, p = t % 2, t // 2
        lines = sizes[o][1] * gz
        recv = one[o][1]
        if sizes[o][0] > 1:
            arrived(recv.at[p], sems1.at[t])
        piece = mine[t, :lines]
        for j in range(1, sizes[o][0]):
            piece = piece + recv[p, j - 1].astype(jnp.float32)
        send, recv = two[o]
        for j in range(1, sizes[o][1]):
            send[p, j - 1] = piece[j * gz:(j + 1) * gz].astype(jnp.bfloat16)
            push(send.at[p, j - 1], recv.at[p, j - 1], send_sems.at[3 + o], sems2.at[t], hops[o][1](j))
        mine[t, :gz] = piece[:gz]

    def third(p):
        pieces = []
        for o in range(2):
            t = 2 * p + o
            recv = two[o][1]
            if sizes[o][1] > 1:
                arrived(recv.at[p], sems2.at[t])
            piece = mine[t, :gz]
            for j in range(1, sizes[o][1]):
                piece = piece + recv[p, j - 1].astype(jnp.float32)
            pieces.append(piece)
        for i in range(1, gz):
            s3[p, i - 1] = jnp.concatenate([piece[i:i + 1] for piece in pieces], axis=0).astype(jnp.bfloat16)
            push(s3.at[p, i - 1], r3.at[p, i - 1], send_sems.at[5], sems3.at[p], z_peer(i))
        own.append(jnp.concatenate([piece[0:1] for piece in pieces], axis=0))

    reach = small_send.shape[2] // 2
    stages = ((1, lambda j: sibling), (gx - 1, x_peer), (gy - 1, y_peer), (gz - 1, z_peer))

    def small_start():
        lane = lax.broadcasted_iota(jnp.int32, (rows, reach), 1).astype(jnp.float32)
        hits = jnp.where(lane == cls_col, 1.0, 0.0)
        small_send[0, :, :reach] = jnp.sum(hits, axis=0, keepdims=True)
        small_send[0, :, reach:] = jnp.sum(hits * sums["wedge"], axis=0, keepdims=True)
        small_push(0)

    def small_push(k):
        at = sum(n for n, _ in stages[:k])
        for j in range(stages[k][0]):
            push(small_send.at[k], small_recv.at[at + j], send_sems.at[6], small_sems.at[k], stages[k][1](j + 1))

    def small_take(k):
        at, n = sum(n for n, _ in stages[:k]), stages[k][0]
        tally = small_send[k]
        if n:
            arrived(small_recv.at[pl.ds(at, n)], small_sems.at[k])
        for j in range(n):
            tally = tally + small_recv[at + j]
        return tally

    def small_next(k):
        small_send[k + 1] = small_take(k)
        small_push(k + 1)

    def score():
        arrived(all_ref.at[pl.ds(half, half)], ag_sems.at[0])
        nt = (((1,), (1,)), ((), ()))
        group = min(classes, 32)
        out = jnp.zeros((rows, classes), jnp.float32)
        power = sums["power"]
        for g in range(classes // group):
            inter = jnp.zeros((rows, group), jnp.float32)
            energy = jnp.zeros((rows, group), jnp.float32)
            lines = slice(g * group, (g + 1) * group)
            for t in range(CHUNKS):
                width = max(0, min(span, coef - t * span))
                if width == 0:
                    continue
                cols = slice(t * span, t * span + width)
                both = jnp.swapaxes(all_ref[lines, :, cols].astype(jnp.float32), 0, 1)
                real, imag = both[0], both[1]
                ref_power = (real * real + imag * imag).astype(jnp.bfloat16)
                inter = inter + lax.dot_general(data[t, :, :width], real.astype(jnp.bfloat16), nt, preferred_element_type=jnp.float32)
                inter = inter + lax.dot_general(data[t, :, span:span + width], imag.astype(jnp.bfloat16), nt, preferred_element_type=jnp.float32)
                energy = energy + lax.dot_general(low[:, cols], ref_power, nt, preferred_element_type=jnp.float32)
            value = inter / (math.sqrt(coef) * jnp.sqrt((energy / coef + EPS) * (power / coef + EPS)))
            lane = lax.broadcasted_iota(jnp.int32, (group, classes), 1)
            place = jnp.where(ids[0][lines] == lane, 1.0, 0.0)
            out = out + jnp.dot(value, place, precision=lax.Precision.HIGHEST, preferred_element_type=jnp.float32)
        scores_ref[...] = out

    def means(p, floor):
        if gz > 1:
            arrived(r3.at[p], sems3.at[p])
        whole = own[p]
        for i in range(1, gz):
            whole = whole + r3[p, i - 1].astype(jnp.float32)
        scale = 1.0 / (whole[:, 2 * span:] + floor)
        for o in range(2):
            start = (2 * p + o) * span
            width = max(0, min(span, coef - start))
            for q in range(2):
                if width:
                    mean = whole[o:o + 1, q * span:q * span + width] * scale[o:o + 1, :width]
                    means_ref[0, q:q + 1, start:start + width] = mean

    compute(0)
    compute(1)
    pl.semaphore_wait(barrier, len(peers))
    cores(0)
    cores(1)
    ag_own()
    compute(2)
    compute(3)
    cores(2)
    cores(3)
    first(0)
    first(1)
    ag_forward(0, 1, 2)
    compute(4)
    compute(5)
    cores(4)
    cores(5)
    small_start()
    first(2)
    first(3)
    ag_core(0, 1, 2)
    first(4)
    first(5)
    ag_rest()
    small_next(0)
    second(0)
    second(1)
    small_next(1)
    second(2)
    second(3)
    third(0)
    small_next(2)
    second(4)
    second(5)
    third(1)
    ag_forward(1, gz - 1, 6)
    third(2)
    ag_core(1, gz - 1, 6)
    score()
    tally = small_take(3)
    load_ref[...] = tally[:, :classes] * classes / total
    lane = lax.broadcasted_iota(jnp.int32, (1, reach), 1)
    wedge_total = jnp.sum(jnp.where(lane == me, tally[:, reach:], 0.0), axis=1, keepdims=True)
    floor = TAU * (wedge_total / coef + 1.0)
    for p in range(PAIRS):
        means(p, floor)

    whole_of(all_ref.at[pl.ds(0, classes - 1)], ag_send_sem).wait_send()
    for ref, at in ((send_core, 0), (s1x, 1), (s1y, 2), (s2x, 3), (s2y, 4), (s3, 5), (small_recv, 6)):
        whole_of(ref, send_sems.at[at]).wait_send()


def finish(*arrays):
    n = len(arrays)

    def put(*refs):
        sems = refs[2 * n]
        copies = [pltpu.make_async_copy(refs[i], refs[n + i], sems.at[i]) for i in range(n)]
        for copy in copies:
            copy.start()
        for copy in copies:
            copy.wait()

    scores, means, load = pl.pallas_call(
        put,
        out_shape=tuple(jax.ShapeDtypeStruct(a.shape, a.dtype) for a in arrays),
        in_specs=[pl.BlockSpec(memory_space=pltpu.VMEM)] * n,
        out_specs=(pl.BlockSpec(memory_space=pltpu.HBM),) * n,
        scratch_shapes=[pltpu.SemaphoreType.DMA((n,))],
        compiler_params=pltpu.CompilerParams(vmem_limit_bytes=1024 * 1024),
    )(*arrays)
    return (scores, means, load[0])


def body(particles, references, assignment, orientation, tilt_range):
    part_rows = particles.shape[0]
    coef = particles.shape[2]
    devices = lax.axis_size("dom")
    classes = references.shape[0] * devices
    assert references.shape[0] == 1
    gx, gy, gz = factor(devices)
    total = part_rows * devices
    span = -(-coef // (CHUNKS * SUB)) * SUB
    padded = CHUNKS * span
    width = 2 * (-(-classes // LANES) * LANES)
    half = classes // 2

    vmem = pl.BlockSpec(memory_space=pltpu.VMEM)
    hbm = pl.BlockSpec(memory_space=pltpu.HBM)
    dma = pltpu.SemaphoreType.DMA
    bf16, f32, i32 = jnp.bfloat16, jnp.float32, jnp.int32
    wide = 3 * span

    def hop(n, lines):
        return [((PAIRS, max(1, n - 1), lines, wide), bf16)] * 2

    buffers = [
        ((part_rows, 2, coef), bf16),
        ((1, part_rows), i32),
        ((1, part_rows), i32),
        ((2, part_rows), i32),
        ((CHUNKS, part_rows, wide), bf16),
        ((part_rows, padded), bf16),
        ((classes, 2, coef), bf16),
        ((CHUNKS, half, wide), f32),
        ((CHUNKS, half, wide), bf16),
        ((CHUNKS, half, wide), bf16),
        *hop(gx, gy * gz), *hop(gy, gx * gz), *hop(gy, gz), *hop(gx, gz), *hop(gz, 2),
        ((4, 1, width), f32),
        ((gx + gy + gz - 2, 1, width), f32),
    ]
    held = sum(math.prod(shape) * jnp.dtype(kind).itemsize for shape, kind in buffers)
    limit = min(60, held // 2**20 + 8) * 2**20
    scores, means, load = pl.pallas_call(
        functools.partial(kernel, gx, gy, gz, span, coef, total),
        out_shape=(
            jax.ShapeDtypeStruct((part_rows, classes), f32),
            jax.ShapeDtypeStruct((1, 2, coef), f32),
            jax.ShapeDtypeStruct((1, classes), f32),
        ),
        in_specs=[hbm] * 5,
        out_specs=(vmem, vmem, vmem),
        scratch_shapes=[pltpu.VMEM(shape, kind) for shape, kind in buffers] + [
            dma((4 + PAIRS,)), dma((10,)), dma, dma((CHUNKS,)), dma((CHUNKS,)), dma((CHUNKS,)), dma((PAIRS,)),
            dma((4,)), dma((7,)),
        ],
        compiler_params=pltpu.CompilerParams(
            collective_id=0, has_side_effects=True, vmem_limit_bytes=limit
        ),
    )(*[
        pltpu.with_memory_space_constraint(v, pltpu.HBM)
        for v in (particles, references, assignment.reshape(1, part_rows), orientation[None, :], tilt_range)
    ])
    return finish(scores, means, load)


def solution(mesh):
    in_specs = (
        P("dom", None, None),
        P("dom", None, None),
        P("dom", None),
        P("dom"),
        P(None, "dom"),
    )
    out_specs = (P("dom", None), P("dom", None, None), P())
    return jax.shard_map(body, mesh=mesh, in_specs=in_specs, out_specs=out_specs, check_vma=False)
```

time: 28.7 us -> 28 us (0.976)
  Pallas kernels: 27.9 us -> 27.2 us
    pallas_call x2, Pallas kernels: 27.9 us -> 27.2 us  [the longest x1 26.5 us: body(): pl.pallas_call(functools.partial(kernel, gx, gy, gz, span, coef, total),...]
where the time goes in v1:
time: 28 us; the launch traced here: 27.8 us
  Pallas kernels  27.2 us (97%)
  between operations  0.64 us (2%)
    pallas_call x1, Pallas kernels, body(): pl.pallas_call(functools.partial(kernel, gx, gy, gz, span, coef, total),...  26.5 us
    pallas_call x1, Pallas kernels, finish(): pl.pallas_call(put, out_shape=tuple((jax.ShapeDtypeStruct(a.shape, a.dtyp...  0.66 us

profile of v1, /device:TPU:0, one launch (start us, length us, event | category | flops | bytes accessed | tf_op | source)
XLA Modules:
  0.0 27.8 jit_solution(14300009864597804436)
XLA Ops:
  0.6 26.5 %shard_map.76 = (f32[32,32]{1,0:T(8,128)S(1)}, f32[1,2,7488]{2,1,0:T(2,128)S(1)}, f32[1,32]{1,0:T(1,128)S(1)}) custom-call(bf16[32,2,7488]{2,1,0:T(2,128)(2,1)} %part_hbm.1, bf16[1,2,7488]{2,1,0:T(2,128)(2,1)} %ref_hbm.1, s32[1,32]{1,0:T(1,128)} %bitcast.3, s32[1,32]{1,0:T(1,128)} %bitcast.4, s32[2,32]{1,0:T(2,128)} %tilt_hbm.1), custom_call_target="tpu_custom_call" | custom-call | tf_op jit(solution)/shard_map/pallas_call | solution.py:480
  27.2 0.7 %shard_map.77 = (f32[32,32]{1,0:T(8,128)}, f32[1,2,7488]{2,1,0:T(2,128)}, f32[1,32]{1,0:T(1,128)}) custom-call(f32[32,32]{1,0:T(8,128)S(1)} %get-tuple-element.9.refs_0_, f32[1,2,7488]{2,1,0:T(2,128)S(1)} %get-tuple-element.10.refs_1_, f32[1,32]{1,0:T(1,128)S(1)} %get-tuple-element.11.refs_2_), custom_call_target="tpu_custom_call" | custom-call | tf_op jit(solution)/shard_map/pallas_call | solution.py:430

commit v2 on v1

--- a/solution.py
+++ b/solution.py
@@ -19,6 +19,8 @@
 PAIRS = 3
 CHUNKS = 2 * PAIRS
 SUB = 640
+ORDERS = ("xzy", "yzx", "xyz", "yxz", "xyz", "yxz")
+SMALL = "xyz"
 
 
 def factor(devices):
@@ -52,10 +54,10 @@
     part_hbm, ref_hbm, cls_hbm, orient_hbm, tilt_hbm,
     scores_ref, means_ref, load_ref,
     part, cls_ref, orient_ref, tilt_ref,
-    data, low, all_ref, mine, send_core, recv_core,
-    s1x, r1x, s1y, r1y, s2x, r2x, s2y, r2y, s3, r3, small_send, small_recv,
-    in_sems, ag_sems, ag_send_sem, core_sems, sems1, sems2, sems3, small_sems, send_sems,
+    data, low, all_ref, mine, send_core, recv_core, small_send, small_recv, *rest,
 ):
+    hop_sends, hop_recvs = rest[:3 * CHUNKS], rest[3 * CHUNKS:6 * CHUNKS]
+    in_sems, ag_sems, core_sems, hop_sems, small_sems, send_sems = rest[6 * CHUNKS:]
     me = lax.axis_index("dom")
     core = lax.rem(me, 2)
     chip = me // 2
@@ -80,6 +82,9 @@
 
     def z_peer(j):
         return device(x, y, lax.rem(z + j, gz), core)
+
+    sizes = {"x": gx, "y": gy, "z": gz}
+    peer_of = {"x": x_peer, "y": y_peer, "z": z_peer}
 
     def fetch(src, dst, at):
         copy = pltpu.make_async_copy(src, dst, in_sems.at[at])
@@ -126,7 +131,7 @@
     def give(src_slot, dst_slot, n, lanes, at, target):
         src = all_ref.at[pl.ds(src_slot, n), :, lanes]
         dst = all_ref.at[pl.ds(dst_slot, n), :, lanes]
-        push(src, dst, ag_send_sem, ag_sems.at[at], target)
+        push(src, dst, send_sems.at[0], ag_sems.at[at], target)
 
     every = slice(0, coef)
     front, back = slice(0, cut), slice(cut, coef)
@@ -190,25 +195,20 @@
         return n.bit_length() - 1
 
     row = lax.broadcasted_iota(jnp.int32, (classes, 1), 0)
-    row_z = row & (gz - 1)
-    up = lax.shift_right_logical(row, log2(gz))
-    row_c = lax.shift_right_logical(row, log2(half))
-
-    def ids_of(dx, dy):
-        return device((dx + x) & (gx - 1), (dy + y) & (gy - 1), (row_z + z) & (gz - 1), (row_c + core) & 1)
-
-    ids = (
-        ids_of(lax.shift_right_logical(up, log2(gy)) & (gx - 1), up & (gy - 1)),
-        ids_of(up & (gx - 1), lax.shift_right_logical(up, log2(gx)) & (gy - 1)),
-    )
-    onehot = [jnp.where(i.astype(jnp.float32) == cls_row, 1.0, 0.0).astype(jnp.bfloat16) for i in ids]
-
-    sizes = ((gx, gy), (gy, gx))
-    hops = ((x_peer, y_peer), (y_peer, x_peer))
-    one = ((s1x, r1x), (s1y, r1y))
-    two = ((s2x, r2x), (s2y, r2y))
+
+    def ids_of(order):
+        left, at = row, {}
+        for dim in reversed(order):
+            at[dim] = left & (sizes[dim] - 1)
+            left = lax.shift_right_logical(left, log2(sizes[dim]))
+        return device((at["x"] + x) & (gx - 1), (at["y"] + y) & (gy - 1), (at["z"] + z) & (gz - 1), (left + core) & 1)
+
+    ids = ids_of("xyz")
+    onehot = {}
+    for order in ORDERS:
+        if order not in onehot:
+            onehot[order] = jnp.where(ids_of(order).astype(jnp.float32) == cls_row, 1.0, 0.0).astype(jnp.bfloat16)
     sums = {"wedge": jnp.zeros((rows, 1), jnp.float32), "power": jnp.zeros((rows, 1), jnp.float32)}
-    own = []
 
     def parts(first):
         width = max(0, min(SUB, coef - first))
@@ -222,8 +222,7 @@
         return both[0], both[1]
 
     def compute(t):
-        o = t % 2
-        if o == 0:
+        if t % 2 == 0:
             part_copies[t // 2].wait()
         for s in range(span // SUB):
             first = t * span + s * SUB
@@ -245,57 +244,56 @@
             low[:, first:first + SUB] = wedge.astype(jnp.bfloat16)
         for q in range(3):
             cols = slice(q * span, (q + 1) * span)
-            both = jnp.dot(onehot[o], data[t, :, cols], preferred_element_type=jnp.float32)
+            both = jnp.dot(onehot[ORDERS[t]], data[t, :, cols], preferred_element_type=jnp.float32)
             send_core[t, :, cols] = both[half:].astype(jnp.bfloat16)
             mine[t, :, cols] = both[:half]
 
     def cores(t):
-        push(send_core.at[t], recv_core.at[t], send_sems.at[0], core_sems.at[t], sibling)
+        push(send_core.at[t], recv_core.at[t], send_sems.at[1], core_sems.at[t], sibling)
+
+    def fold(line):
+        return jnp.concatenate([line[:, :wide // 2], line[:, wide // 2:]], axis=0)
+
+    def taken(t, k):
+        if k < 0:
+            arrived(recv_core.at[t], core_sems.at[t])
+            return mine[t] + recv_core[t].astype(jnp.float32)
+        n = sizes[ORDERS[t][k]]
+        lines = math.prod(sizes[dim] for dim in ORDERS[t][k + 1:])
+        piece = mine[t, :lines]
+        if lines == 1:
+            piece = fold(piece)
+        recv = hop_recvs[3 * t + k]
+        if n > 1:
+            arrived(recv, hop_sems.at[3 * t + k])
+        for j in range(1, n):
+            piece = piece + recv[j - 1].astype(jnp.float32)
+        return piece
+
+    def hop(t, k):
+        dim = ORDERS[t][k]
+        lines = math.prod(sizes[dim] for dim in ORDERS[t][k + 1:])
+        piece = taken(t, k - 1)
+        send, recv = hop_sends[3 * t + k], hop_recvs[3 * t + k]
+        for j in range(1, sizes[dim]):
+            part_of = piece[j * lines:(j + 1) * lines]
+            if lines == 1:
+                part_of = fold(part_of)
+            send[j - 1] = part_of.astype(jnp.bfloat16)
+            push(send.at[j - 1], recv.at[j - 1], send_sems.at[2], hop_sems.at[3 * t + k], peer_of[dim](j))
+        mine[t, :lines] = piece[:lines]
 
     def first(t):
-        o, p = t % 2, t // 2
-        send, recv = one[o]
-        lines = sizes[o][1] * gz
-        arrived(recv_core.at[t], core_sems.at[t])
-        for j in range(1, sizes[o][0]):
-            at = slice(j * lines, (j + 1) * lines)
-            send[p, j - 1] = (mine[t, at] + recv_core[t, at].astype(jnp.float32)).astype(jnp.bfloat16)
-            push(send.at[p, j - 1], recv.at[p, j - 1], send_sems.at[1 + o], sems1.at[t], hops[o][0](j))
-        mine[t, :lines] = mine[t, :lines] + recv_core[t, :lines].astype(jnp.float32)
+        hop(t, 0)
 
     def second(t):
-        o, p = t % 2, t // 2
-        lines = sizes[o][1] * gz
-        recv = one[o][1]
-        if sizes[o][0] > 1:
-            arrived(recv.at[p], sems1.at[t])
-        piece = mine[t, :lines]
-        for j in range(1, sizes[o][0]):
-            piece = piece + recv[p, j - 1].astype(jnp.float32)
-        send, recv = two[o]
-        for j in range(1, sizes[o][1]):
-            send[p, j - 1] = piece[j * gz:(j + 1) * gz].astype(jnp.bfloat16)
-            push(send.at[p, j - 1], recv.at[p, j - 1], send_sems.at[3 + o], sems2.at[t], hops[o][1](j))
-        mine[t, :gz] = piece[:gz]
-
-    def third(p):
-        pieces = []
-        for o in range(2):
-            t = 2 * p + o
-            recv = two[o][1]
-            if sizes[o][1] > 1:
-                arrived(recv.at[p], sems2.at[t])
-            piece = mine[t, :gz]
-            for j in range(1, sizes[o][1]):
-                piece = piece + recv[p, j - 1].astype(jnp.float32)
-            pieces.append(piece)
-        for i in range(1, gz):
-            s3[p, i - 1] = jnp.concatenate([piece[i:i + 1] for piece in pieces], axis=0).astype(jnp.bfloat16)
-            push(s3.at[p, i - 1], r3.at[p, i - 1], send_sems.at[5], sems3.at[p], z_peer(i))
-        own.append(jnp.concatenate([piece[0:1] for piece in pieces], axis=0))
+        hop(t, 1)
+
+    def third(t):
+        hop(t, 2)
 
     reach = small_send.shape[2] // 2
-    stages = ((1, lambda j: sibling), (gx - 1, x_peer), (gy - 1, y_peer), (gz - 1, z_peer))
+    stages = [(1, lambda j: sibling)] + [(sizes[dim] - 1, peer_of[dim]) for dim in SMALL]
 
     def small_start():
         lane = lax.broadcasted_iota(jnp.int32, (rows, reach), 1).astype(jnp.float32)
@@ -307,7 +305,7 @@
     def small_push(k):
         at = sum(n for n, _ in stages[:k])
         for j in range(stages[k][0]):
-            push(small_send.at[k], small_recv.at[at + j], send_sems.at[6], small_sems.at[k], stages[k][1](j + 1))
+            push(small_send.at[k], small_recv.at[at + j], send_sems.at[3], small_sems.at[k], stages[k][1](j + 1))
 
     def small_take(k):
         at, n = sum(n for n, _ in stages[:k]), stages[k][0]
@@ -345,62 +343,61 @@
                 energy = energy + lax.dot_general(low[:, cols], ref_power, nt, preferred_element_type=jnp.float32)
             value = inter / (math.sqrt(coef) * jnp.sqrt((energy / coef + EPS) * (power / coef + EPS)))
             lane = lax.broadcasted_iota(jnp.int32, (group, classes), 1)
-            place = jnp.where(ids[0][lines] == lane, 1.0, 0.0)
+            place = jnp.where(ids[lines] == lane, 1.0, 0.0)
             out = out + jnp.dot(value, place, precision=lax.Precision.HIGHEST, preferred_element_type=jnp.float32)
         scores_ref[...] = out
 
-    def means(p, floor):
-        if gz > 1:
-            arrived(r3.at[p], sems3.at[p])
-        whole = own[p]
-        for i in range(1, gz):
-            whole = whole + r3[p, i - 1].astype(jnp.float32)
-        scale = 1.0 / (whole[:, 2 * span:] + floor)
-        for o in range(2):
-            start = (2 * p + o) * span
-            width = max(0, min(span, coef - start))
-            for q in range(2):
-                if width:
-                    mean = whole[o:o + 1, q * span:q * span + width] * scale[o:o + 1, :width]
-                    means_ref[0, q:q + 1, start:start + width] = mean
+    def means(t, floor):
+        whole = taken(t, 2)
+        flat = jnp.concatenate([whole[0:1], whole[1:2]], axis=1)
+        start = t * span
+        width = max(0, min(span, coef - start))
+        if width == 0:
+            return
+        scale = 1.0 / (flat[:, 2 * span:2 * span + width] + floor)
+        for q in range(2):
+            means_ref[0, q:q + 1, start:start + width] = flat[:, q * span:q * span + width] * scale
 
     compute(0)
+    pl.semaphore_wait(barrier, len(peers))
+    ag_own()
+    cores(0)
     compute(1)
-    pl.semaphore_wait(barrier, len(peers))
-    cores(0)
     cores(1)
-    ag_own()
     compute(2)
+    cores(2)
     compute(3)
-    cores(2)
     cores(3)
-    first(0)
-    first(1)
-    ag_forward(0, 1, 2)
+    hop(0, 0)
+    hop(1, 0)
     compute(4)
+    cores(4)
     compute(5)
-    cores(4)
     cores(5)
     small_start()
-    first(2)
-    first(3)
+    hop(2, 0)
+    hop(3, 0)
+    ag_forward(0, 1, 2)
+    hop(4, 0)
+    hop(5, 0)
+    small_next(0)
+    hop(0, 1)
+    hop(1, 1)
+    ag_rest()
     ag_core(0, 1, 2)
-    first(4)
-    first(5)
-    ag_rest()
-    small_next(0)
-    second(0)
-    second(1)
+    hop(2, 1)
+    hop(3, 1)
+    hop(4, 1)
+    hop(5, 1)
     small_next(1)
-    second(2)
-    second(3)
-    third(0)
+    hop(0, 2)
+    hop(1, 2)
+    ag_forward(1, gz - 1, 6)
+    hop(2, 2)
+    hop(3, 2)
+    hop(4, 2)
+    hop(5, 2)
     small_next(2)
-    second(4)
-    second(5)
-    third(1)
-    ag_forward(1, gz - 1, 6)
-    third(2)
     ag_core(1, gz - 1, 6)
     score()
     tally = small_take(3)
@@ -408,12 +405,13 @@
     lane = lax.broadcasted_iota(jnp.int32, (1, reach), 1)
     wedge_total = jnp.sum(jnp.where(lane == me, tally[:, reach:], 0.0), axis=1, keepdims=True)
     floor = TAU * (wedge_total / coef + 1.0)
-    for p in range(PAIRS):
-        means(p, floor)
-
-    whole_of(all_ref.at[pl.ds(0, classes - 1)], ag_send_sem).wait_send()
-    for ref, at in ((send_core, 0), (s1x, 1), (s1y, 2), (s2x, 3), (s2y, 4), (s3, 5), (small_recv, 6)):
-        whole_of(ref, send_sems.at[at]).wait_send()
+    for t in range(CHUNKS):
+        means(t, floor)
+
+    whole_of(all_ref.at[pl.ds(0, classes - 1)], send_sems.at[0]).wait_send()
+    whole_of(send_core, send_sems.at[1]).wait_send()
+    whole_of(all_ref.at[pl.ds(0, classes - 2), :, :CHUNKS * wide // 4], send_sems.at[2]).wait_send()
+    whole_of(small_recv, send_sems.at[3]).wait_send()
 
 
 def finish(*arrays):
@@ -457,9 +455,13 @@
     bf16, f32, i32 = jnp.bfloat16, jnp.float32, jnp.int32
     wide = 3 * span
 
-    def hop(n, lines):
-        return [((PAIRS, max(1, n - 1), lines, wide), bf16)] * 2
-
+    sizes = {"x": gx, "y": gy, "z": gz}
+    hops = []
+    for order in ORDERS:
+        for k, dim in enumerate(order):
+            lines = math.prod(sizes[d] for d in order[k + 1:])
+            shape = (lines, wide) if lines > 1 else (2, wide // 2)
+            hops.append(((max(1, sizes[dim] - 1), *shape), bf16))
     buffers = [
         ((part_rows, 2, coef), bf16),
         ((1, part_rows), i32),
@@ -471,9 +473,9 @@
         ((CHUNKS, half, wide), f32),
         ((CHUNKS, half, wide), bf16),
         ((CHUNKS, half, wide), bf16),
-        *hop(gx, gy * gz), *hop(gy, gx * gz), *hop(gy, gz), *hop(gx, gz), *hop(gz, 2),
         ((4, 1, width), f32),
         ((gx + gy + gz - 2, 1, width), f32),
+        *hops, *hops,
     ]
     held = sum(math.prod(shape) * jnp.dtype(kind).itemsize for shape, kind in buffers)
     limit = min(60, held // 2**20 + 8) * 2**20
@@ -487,8 +489,7 @@
         in_specs=[hbm] * 5,
         out_specs=(vmem, vmem, vmem),
         scratch_shapes=[pltpu.VMEM(shape, kind) for shape, kind in buffers] + [
-            dma((4 + PAIRS,)), dma((10,)), dma, dma((CHUNKS,)), dma((CHUNKS,)), dma((CHUNKS,)), dma((PAIRS,)),
-            dma((4,)), dma((7,)),
+            dma((4 + PAIRS,)), dma((10,)), dma((CHUNKS,)), dma((3 * CHUNKS,)), dma((4,)), dma((4,)),
         ],
         compiler_params=pltpu.CompilerParams(
             collective_id=0, has_side_effects=True, vmem_limit_bytes=limit

time: 28 us -> 23.4 us (0.84)
  the two profiles are of different devices: /device:TPU:0 before, /device:TPU:1 now
where the time goes in v2:
time: 23.4 us; the launch traced here: 23.2 us
  Pallas kernels  22.6 us (97%)
  between operations  0.64 us (3%)
    pallas_call x1, Pallas kernels, body(): pl.pallas_call(functools.partial(kernel, gx, gy, gz, span, coef, total),...  21.9 us
    pallas_call x1, Pallas kernels, finish(): pl.pallas_call(put, out_shape=tuple((jax.ShapeDtypeStruct(a.shape, a.dtyp...  0.66 us

profile of v2, /device:TPU:1, one launch (start us, length us, event | category | flops | bytes accessed | tf_op | source)
XLA Modules:
  0.0 23.2 jit_solution(17101896555770771377)
XLA Ops:
  0.6 21.9 %shard_map.76 = (f32[32,32]{1,0:T(8,128)S(1)}, f32[1,2,7488]{2,1,0:T(2,128)S(1)}, f32[1,32]{1,0:T(1,128)S(1)}) custom-call(bf16[32,2,7488]{2,1,0:T(2,128)(2,1)} %part_hbm.1, bf16[1,2,7488]{2,1,0:T(2,128)(2,1)} %ref_hbm.1, s32[1,32]{1,0:T(1,128)} %bitcast.3, s32[1,32]{1,0:T(1,128)} %bitcast.4, s32[2,32]{1,0:T(2,128)} %tilt_hbm.1), custom_call_target="tpu_custom_call" | custom-call | tf_op jit(solution)/shard_map/pallas_call | solution.py:482
  22.5 0.7 %shard_map.77 = (f32[32,32]{1,0:T(8,128)}, f32[1,2,7488]{2,1,0:T(2,128)}, f32[1,32]{1,0:T(1,128)}) custom-call(f32[32,32]{1,0:T(8,128)S(1)} %get-tuple-element.9.refs_0_, f32[1,2,7488]{2,1,0:T(2,128)S(1)} %get-tuple-element.10.refs_1_, f32[1,32]{1,0:T(1,128)S(1)} %get-tuple-element.11.refs_2_), custom_call_target="tpu_custom_call" | custom-call | tf_op jit(solution)/shard_map/pallas_call | solution.py:428

commit v3 on v2

--- a/solution.py
+++ b/solution.py
@@ -16,11 +16,12 @@
 LANES = 128
 MESH = pl.DeviceIdType.MESH
 
-PAIRS = 3
-CHUNKS = 2 * PAIRS
+SHARES = (10, 10, 10, 10, 10, 10)
+CHUNKS = len(SHARES)
 SUB = 640
 ORDERS = ("xzy", "yzx", "xyz", "yxz", "xyz", "yxz")
 SMALL = "xyz"
+PIECES = 3
 
 
 def factor(devices):
@@ -29,6 +30,13 @@
     gx = 1 << (log // 3)
     gy = 1 << ((log - log // 3) // 2)
     return gx, gy, chips // (gx * gy)
+
+
+def spans_of(coef):
+    unit = sum(SHARES)
+    pairs = -(-coef // (4 * LANES)) * 2
+    ends = [sum(SHARES[:t + 1]) * pairs // unit for t in range(CHUNKS)]
+    return [(end - start) * 2 * LANES for start, end in zip([0] + ends, ends)]
 
 
 def column(row):
@@ -50,14 +58,17 @@
 
 
 def kernel(
-    gx, gy, gz, span, coef, total,
+    gx, gy, gz, spans, coef, total,
     part_hbm, ref_hbm, cls_hbm, orient_hbm, tilt_hbm,
     scores_ref, means_ref, load_ref,
     part, cls_ref, orient_ref, tilt_ref,
-    data, low, all_ref, mine, send_core, recv_core, small_send, small_recv, *rest,
+    low, all_ref, ready, small_send, small_recv, *rest,
 ):
     hop_sends, hop_recvs = rest[:3 * CHUNKS], rest[3 * CHUNKS:6 * CHUNKS]
-    in_sems, ag_sems, core_sems, hop_sems, small_sems, send_sems = rest[6 * CHUNKS:]
+    data, mine, send_core, recv_core = (rest[k * CHUNKS:(k + 1) * CHUNKS] for k in range(6, 10))
+    in_sems, ag_sems, core_sems, hop_sems, small_sems, send_sems = rest[10 * CHUNKS:]
+    starts = [sum(spans[:t]) for t in range(CHUNKS)]
+    widths = [max(0, min(spans[t], coef - starts[t])) for t in range(CHUNKS)]
     me = lax.axis_index("dom")
     core = lax.rem(me, 2)
     chip = me // 2
@@ -68,7 +79,6 @@
     classes = 2 * gx * gy * gz
     half = classes // 2
     rows = part.shape[0]
-    wide = 3 * span
     cut = coef // 2 // LANES * LANES
 
     def device(x_at, y_at, z_at, c_at):
@@ -79,6 +89,12 @@
 
     def y_peer(j):
         return device(x, lax.rem(y + j, gy), z, core)
+
+    def x_cross(j):
+        return device(lax.rem(x + j, gx), y, z, 1 - core)
+
+    def y_cross(j):
+        return device(x, lax.rem(y + j, gy), z, 1 - core)
 
     def z_peer(j):
         return device(x, y, lax.rem(z + j, gz), core)
@@ -96,19 +112,20 @@
     peers += [x_peer(j) for j in range(1, gx)]
     peers += [y_peer(j) for j in range(1, gy)]
     peers += [z_peer(j) for j in range(1, gz)]
+    peers += [x_cross(j) for j in range(1, gx)]
+    peers += [y_cross(j) for j in range(1, gy)]
     for peer in peers:
         pl.semaphore_signal(barrier, inc=1, device_id=(peer,), device_id_type=MESH)
-    own_ref = fetch(ref_hbm.at[0], all_ref.at[0], 0)
     metas = [
         fetch(orient_hbm, orient_ref, 1),
         fetch(tilt_hbm, tilt_ref, 2),
         fetch(cls_hbm, cls_ref, 3),
     ]
+    own_ref = fetch(ref_hbm.at[0], all_ref.at[0], 0)
     part_copies = []
-    for p in range(PAIRS):
-        first = 2 * p * span
-        cols = pl.ds(first, min(2 * span, coef - first))
-        part_copies.append(fetch(part_hbm.at[:, :, cols], part.at[:, :, cols], 4 + p))
+    for t in range(CHUNKS):
+        cols = pl.ds(starts[t], widths[t])
+        part_copies.append(fetch(part_hbm.at[:, :, cols], part.at[:, :, cols], 4 + t))
 
     def push(src, dst, send_sem, recv_sem, target):
         pltpu.make_async_remote_copy(
@@ -136,47 +153,83 @@
     every = slice(0, coef)
     front, back = slice(0, cut), slice(cut, coef)
 
-    def ag_direct(at, n, sem):
+    def split(g):
+        return 1 + g * (gz - 1) // PIECES, 1 + (g + 1) * (gz - 1) // PIECES
+
+    def sem_of(g):
+        return 3 + 4 * (g + 1)
+
+    cross = sem_of(PIECES)
+
+    def ag_direct(g):
+        at, end = split(g) if g >= 0 else (0, 1)
+        sem = sem_of(g)
+        if at == end:
+            return
         for j in range(1, gx):
-            give(at, slot(gx - j, 0, 0) + at, n, every, sem, x_peer(j))
+            give(at, slot(gx - j, 0, 0) + at, end - at, every, sem, x_peer(j))
         for j in range(1, gy):
-            give(at, slot(0, gy - j, 0) + at, n, every, sem + 1, y_peer(j))
-        give(at, slot(0, 0, 1) + at, n, every, 0, sibling)
-
-    def ag_forward(at, n, sem):
+            give(at, slot(0, gy - j, 0) + at, end - at, every, sem + 1, y_peer(j))
+        give(at, slot(0, 0, 1) + at, end - at, every, 0, sibling)
+
+    def ag_forward(g):
+        at, end = split(g) if g >= 0 else (0, 1)
+        n, sem = end - at, sem_of(g)
+        if n == 0:
+            return
         if gx > 1:
             arrived(all_ref.at[pl.ds(0, (gx - 1) * n)], ag_sems.at[sem])
         for dx in range(1, gx):
             for j in range(1, gy):
                 give(slot(dx, 0, 0) + at, slot(dx, gy - j, 0) + at, n, front, sem + 2, y_peer(j))
+                if g == PIECES - 1:
+                    give(slot(dx, 0, 0) + at, slot(dx, gy - j, 1) + at, n, front, cross, y_cross(j))
         if gy > 1:
             arrived(all_ref.at[pl.ds(0, (gy - 1) * n)], ag_sems.at[sem + 1])
         for dy in range(1, gy):
             for j in range(1, gx):
                 give(slot(0, dy, 0) + at, slot(gx - j, dy, 0) + at, n, back, sem + 3, x_peer(j))
+                if g == PIECES - 1:
+                    give(slot(0, dy, 0) + at, slot(gx - j, dy, 1) + at, n, back, cross + 1, x_cross(j))
         for dx in range(1, gx):
             give(slot(dx, 0, 0) + at, slot(dx, 0, 1) + at, n, every, 0, sibling)
         for dy in range(1, gy):
             give(slot(0, dy, 0) + at, slot(0, dy, 1) + at, n, every, 0, sibling)
 
-    def ag_core(at, n, sem):
+    def ag_core(g):
+        at, end = split(g) if g >= 0 else (0, 1)
+        n, sem = end - at, sem_of(g)
         count = (gx - 1) * (gy - 1) * n
         if count:
             arrived(all_ref.at[pl.ds(0, count), :, front], ag_sems.at[sem + 2])
             arrived(all_ref.at[pl.ds(0, count), :, back], ag_sems.at[sem + 3])
+        if g == PIECES - 1:
+            return
         for dx in range(1, gx):
             for dy in range(1, gy):
-                give(slot(dx, dy, 0) + at, slot(dx, dy, 1) + at, n, every, 0, sibling)
+                give(slot(dx, dy, 0) + at, slot(dx, dy, 1) + at, n, every, 1, sibling)
 
     def ag_own():
         own_ref.wait()
         for j in range(1, gz):
-            give(0, gz - j, 1, every, 1, z_peer(j))
-        ag_direct(0, 1, 2)
-
-    def ag_rest():
-        arrived(all_ref.at[pl.ds(1, gz - 1)], ag_sems.at[1])
-        ag_direct(1, gz - 1, 6)
+            give(0, gz - j, 1, every, 2, z_peer(j))
+        ag_direct(-1)
+
+    def ag_z():
+        if gz > 1:
+            arrived(all_ref.at[pl.ds(1, gz - 1)], ag_sems.at[2])
+
+    diag = (gx - 1) * (gy - 1) * gz
+    early, late = [], []
+    for dc in range(2):
+        for dx in range(gx):
+            for dy in range(gy):
+                runs = late if dx and dy else early
+                at = slot(dx, dy, dc)
+                if runs and runs[-1][1] == at and at != half:
+                    runs[-1] = (runs[-1][0], at + gz)
+                else:
+                    runs.append((at, at + gz))
 
     for copy in metas:
         copy.wait()
@@ -210,57 +263,62 @@
             onehot[order] = jnp.where(ids_of(order).astype(jnp.float32) == cls_row, 1.0, 0.0).astype(jnp.bfloat16)
     sums = {"wedge": jnp.zeros((rows, 1), jnp.float32), "power": jnp.zeros((rows, 1), jnp.float32)}
 
-    def parts(first):
-        width = max(0, min(SUB, coef - first))
+    def parts(first, size):
+        width = max(0, min(size, coef - first))
         pieces = []
         if width:
             both = part[:, :, first:first + width].astype(jnp.float32)
             pieces.append(jnp.swapaxes(both, 0, 1))
-        if width < SUB:
-            pieces.append(jnp.zeros((2, rows, SUB - width), jnp.float32))
+        if width < size:
+            pieces.append(jnp.zeros((2, rows, size - width), jnp.float32))
         both = jnp.concatenate(pieces, axis=2) if len(pieces) > 1 else pieces[0]
         return both[0], both[1]
 
+    def wedges(first, size):
+        freq_x, freq_y, freq_z, index = frequencies(first, size)
+        along = freq_y * cos_a - freq_x * sin_a
+        along_sq = along * along
+        z_sq = freq_z * freq_z
+        scale = 1.0 / (along_sq + (z_sq + 1.0))
+        value = ((along_sq - z_sq) * cos_c - (2.0 * along * freq_z) * sin_c) * scale - cos_w
+        wedge = 1.0 / (1.0 + jnp.exp(value * (-GAIN)))
+        inside = wedge if first + size <= coef else jnp.where(index < coef, wedge, 0.0)
+        sums["wedge"] = sums["wedge"] + jnp.sum(inside, axis=1, keepdims=True)
+        return wedge
+
     def compute(t):
-        if t % 2 == 0:
-            part_copies[t // 2].wait()
-        for s in range(span // SUB):
-            first = t * span + s * SUB
-            freq_x, freq_y, freq_z, index = frequencies(first, SUB)
-            along = freq_y * cos_a - freq_x * sin_a
-            along_sq = along * along
-            z_sq = freq_z * freq_z
-            scale = 1.0 / (along_sq + (z_sq + 1.0))
-            value = ((along_sq - z_sq) * cos_c - (2.0 * along * freq_z) * sin_c) * scale - cos_w
-            wedge = 1.0 / (1.0 + jnp.exp(value * (-GAIN)))
-            real, imag = parts(first)
+        span = spans[t]
+        part_copies[t].wait()
+        for at in range(0, span, SUB):
+            first = starts[t] + at
+            size = min(SUB, span - at)
+            wedge = wedges(first, size)
+            real, imag = parts(first, size)
             sums["power"] = sums["power"] + jnp.sum(wedge * (real * real + imag * imag), axis=1, keepdims=True)
-            inside = wedge if first + SUB <= coef else jnp.where(index < coef, wedge, 0.0)
-            sums["wedge"] = sums["wedge"] + jnp.sum(inside, axis=1, keepdims=True)
-            at = s * SUB
-            data[t, :, at:at + SUB] = (wedge * real).astype(jnp.bfloat16)
-            data[t, :, span + at:span + at + SUB] = (wedge * imag).astype(jnp.bfloat16)
-            data[t, :, 2 * span + at:2 * span + at + SUB] = (wedge * wedge).astype(jnp.bfloat16)
-            low[:, first:first + SUB] = wedge.astype(jnp.bfloat16)
+            data[t][:, at:at + size] = (wedge * real).astype(jnp.bfloat16)
+            data[t][:, span + at:span + at + size] = (wedge * imag).astype(jnp.bfloat16)
+            data[t][:, 2 * span + at:2 * span + at + size] = (wedge * wedge).astype(jnp.bfloat16)
+            low[:, first:first + size] = wedge.astype(jnp.bfloat16)
         for q in range(3):
             cols = slice(q * span, (q + 1) * span)
-            both = jnp.dot(onehot[ORDERS[t]], data[t, :, cols], preferred_element_type=jnp.float32)
-            send_core[t, :, cols] = both[half:].astype(jnp.bfloat16)
-            mine[t, :, cols] = both[:half]
+            both = jnp.dot(onehot[ORDERS[t]], data[t][:, cols], preferred_element_type=jnp.float32)
+            send_core[t][:, cols] = both[half:].astype(jnp.bfloat16)
+            mine[t][:, cols] = both[:half]
 
     def cores(t):
-        push(send_core.at[t], recv_core.at[t], send_sems.at[1], core_sems.at[t], sibling)
+        push(send_core[t], recv_core[t], send_sems.at[1], core_sems.at[t], sibling)
 
     def fold(line):
+        wide = line.shape[1]
         return jnp.concatenate([line[:, :wide // 2], line[:, wide // 2:]], axis=0)
 
     def taken(t, k):
         if k < 0:
-            arrived(recv_core.at[t], core_sems.at[t])
-            return mine[t] + recv_core[t].astype(jnp.float32)
+            arrived(recv_core[t], core_sems.at[t])
+            return mine[t][...] + recv_core[t][...].astype(jnp.float32)
         n = sizes[ORDERS[t][k]]
         lines = math.prod(sizes[dim] for dim in ORDERS[t][k + 1:])
-        piece = mine[t, :lines]
+        piece = mine[t][:lines]
         if lines == 1:
             piece = fold(piece)
         recv = hop_recvs[3 * t + k]
@@ -281,7 +339,7 @@
                 part_of = fold(part_of)
             send[j - 1] = part_of.astype(jnp.bfloat16)
             push(send.at[j - 1], recv.at[j - 1], send_sems.at[2], hop_sems.at[3 * t + k], peer_of[dim](j))
-        mine[t, :lines] = piece[:lines]
+        mine[t][:lines] = piece[:lines]
 
     def first(t):
         hop(t, 0)
@@ -320,41 +378,78 @@
         small_send[k + 1] = small_take(k)
         small_push(k + 1)
 
-    def score():
-        arrived(all_ref.at[pl.ds(half, half)], ag_sems.at[0])
-        nt = (((1,), (1,)), ((), ()))
-        group = min(classes, 32)
-        out = jnp.zeros((rows, classes), jnp.float32)
+    nt = (((1,), (1,)), ((), ()))
+    table = []
+
+    def position(at):
+        before = 0
+        for begin, end in early + late:
+            if begin <= at < end:
+                return before + at - begin
+            before += end - begin
+
+    order = jnp.concatenate([ids[begin:end] for begin, end in early + late], axis=0)
+
+    def prepare(runs):
+        for begin, end in runs:
+            lines = slice(begin, end)
+            for t in range(CHUNKS):
+                cols = slice(starts[t], starts[t] + widths[t])
+                both = jnp.swapaxes(all_ref[lines, :, cols].astype(jnp.float32), 0, 1)
+                real, imag = both[0], both[1]
+                to = slice(position(begin), position(begin) + end - begin)
+                ready[0, to, cols] = real.astype(jnp.bfloat16)
+                ready[1, to, cols] = imag.astype(jnp.bfloat16)
+                ready[2, to, cols] = (real * real + imag * imag).astype(jnp.bfloat16)
+
+    def score(begin, end):
         power = sums["power"]
-        for g in range(classes // group):
+        for at in range(begin, end, 32):
+            lines = slice(at, min(at + 32, end))
+            group = lines.stop - lines.start
             inter = jnp.zeros((rows, group), jnp.float32)
             energy = jnp.zeros((rows, group), jnp.float32)
-            lines = slice(g * group, (g + 1) * group)
             for t in range(CHUNKS):
-                width = max(0, min(span, coef - t * span))
-                if width == 0:
-                    continue
-                cols = slice(t * span, t * span + width)
-                both = jnp.swapaxes(all_ref[lines, :, cols].astype(jnp.float32), 0, 1)
-                real, imag = both[0], both[1]
-                ref_power = (real * real + imag * imag).astype(jnp.bfloat16)
-                inter = inter + lax.dot_general(data[t, :, :width], real.astype(jnp.bfloat16), nt, preferred_element_type=jnp.float32)
-                inter = inter + lax.dot_general(data[t, :, span:span + width], imag.astype(jnp.bfloat16), nt, preferred_element_type=jnp.float32)
-                energy = energy + lax.dot_general(low[:, cols], ref_power, nt, preferred_element_type=jnp.float32)
+                width, span = widths[t], spans[t]
+                cols = slice(starts[t], starts[t] + width)
+                inter = inter + lax.dot_general(data[t][:, :width], ready[0, lines, cols], nt, preferred_element_type=jnp.float32)
+                inter = inter + lax.dot_general(data[t][:, span:span + width], ready[1, lines, cols], nt, preferred_element_type=jnp.float32)
+                energy = energy + lax.dot_general(low[:, cols], ready[2, lines, cols], nt, preferred_element_type=jnp.float32)
             value = inter / (math.sqrt(coef) * jnp.sqrt((energy / coef + EPS) * (power / coef + EPS)))
             lane = lax.broadcasted_iota(jnp.int32, (group, classes), 1)
-            place = jnp.where(ids[lines] == lane, 1.0, 0.0)
-            out = out + jnp.dot(value, place, precision=lax.Precision.HIGHEST, preferred_element_type=jnp.float32)
-        scores_ref[...] = out
-
-    def means(t, floor):
+            place = jnp.where(order[lines] == lane, 1.0, 0.0)
+            table.append(jnp.dot(value, place, precision=lax.Precision.HIGHEST, preferred_element_type=jnp.float32))
+
+    def score_early():
+        prepare([(begin, end) for begin, end in early if end <= half])
+        arrived(all_ref.at[pl.ds(0, half - diag)], ag_sems.at[0])
+        prepare([(begin, end) for begin, end in early if end > half])
+
+    def score_late():
+        last = (gx - 1) * (gy - 1) * (gz - split(PIECES - 1)[0])
+        if diag > last:
+            arrived(all_ref.at[pl.ds(0, diag - last)], ag_sems.at[1])
+        if last:
+            arrived(all_ref.at[pl.ds(0, last), :, front], ag_sems.at[cross])
+            arrived(all_ref.at[pl.ds(0, last), :, back], ag_sems.at[cross + 1])
+        prepare(late)
+        score(classes - 2 * diag, classes)
+        scores_ref[...] = sum(table[1:], table[0])
+
+    floors = []
+
+    def counts():
+        tally = small_take(3)
+        load_ref[...] = tally[:, :classes] * classes / total
+        lane = lax.broadcasted_iota(jnp.int32, (1, reach), 1)
+        wedge_total = jnp.sum(jnp.where(lane == me, tally[:, reach:], 0.0), axis=1, keepdims=True)
+        floors.append(TAU * (wedge_total / coef + 1.0))
+
+    def means(t):
         whole = taken(t, 2)
         flat = jnp.concatenate([whole[0:1], whole[1:2]], axis=1)
-        start = t * span
-        width = max(0, min(span, coef - start))
-        if width == 0:
-            return
-        scale = 1.0 / (flat[:, 2 * span:2 * span + width] + floor)
+        span, width, start = spans[t], widths[t], starts[t]
+        scale = 1.0 / (flat[:, 2 * span:2 * span + width] + floors[0])
         for q in range(2):
             means_ref[0, q:q + 1, start:start + width] = flat[:, q * span:q * span + width] * scale
 
@@ -377,40 +472,49 @@
     small_start()
     hop(2, 0)
     hop(3, 0)
-    ag_forward(0, 1, 2)
+    ag_forward(-1)
+    small_next(0)
     hop(4, 0)
     hop(5, 0)
-    small_next(0)
     hop(0, 1)
     hop(1, 1)
-    ag_rest()
-    ag_core(0, 1, 2)
+    ag_z()
+    ag_direct(0)
+    ag_direct(1)
+    ag_direct(2)
+    ag_core(-1)
     hop(2, 1)
     hop(3, 1)
+    small_next(1)
     hop(4, 1)
     hop(5, 1)
-    small_next(1)
+    ag_forward(0)
     hop(0, 2)
     hop(1, 2)
-    ag_forward(1, gz - 1, 6)
+    ag_forward(1)
+    ag_forward(2)
+    small_next(2)
     hop(2, 2)
     hop(3, 2)
     hop(4, 2)
     hop(5, 2)
-    small_next(2)
-    ag_core(1, gz - 1, 6)
-    score()
-    tally = small_take(3)
-    load_ref[...] = tally[:, :classes] * classes / total
-    lane = lax.broadcasted_iota(jnp.int32, (1, reach), 1)
-    wedge_total = jnp.sum(jnp.where(lane == me, tally[:, reach:], 0.0), axis=1, keepdims=True)
-    floor = TAU * (wedge_total / coef + 1.0)
-    for t in range(CHUNKS):
-        means(t, floor)
+    score_early()
+    ag_core(0)
+    ag_core(1)
+    score(0, classes - 2 * diag)
+    ag_core(2)
+    score_late()
+    counts()
+    means(0)
+    means(1)
+    means(2)
+    means(3)
+    means(4)
+    means(5)
 
     whole_of(all_ref.at[pl.ds(0, classes - 1)], send_sems.at[0]).wait_send()
-    whole_of(send_core, send_sems.at[1]).wait_send()
-    whole_of(all_ref.at[pl.ds(0, classes - 2), :, :CHUNKS * wide // 4], send_sems.at[2]).wait_send()
+    whole_of(ready.at[:, :half, :], send_sems.at[1]).wait_send()
+    whole_of(all_ref.at[pl.ds(0, classes - 2), :, :3 * sum(spans) // 4], send_sems.at[2]).wait_send()
     whole_of(small_recv, send_sems.at[3]).wait_send()
 
 
@@ -444,8 +548,8 @@
     assert references.shape[0] == 1
     gx, gy, gz = factor(devices)
     total = part_rows * devices
-    span = -(-coef // (CHUNKS * SUB)) * SUB
-    padded = CHUNKS * span
+    spans = spans_of(coef)
+    padded = sum(spans)
     width = 2 * (-(-classes // LANES) * LANES)
     half = classes // 2
 
@@ -453,11 +557,11 @@
     hbm = pl.BlockSpec(memory_space=pltpu.HBM)
     dma = pltpu.SemaphoreType.DMA
     bf16, f32, i32 = jnp.bfloat16, jnp.float32, jnp.int32
-    wide = 3 * span
 
     sizes = {"x": gx, "y": gy, "z": gz}
     hops = []
-    for order in ORDERS:
+    for order, span in zip(ORDERS, spans):
+        wide = 3 * span
         for k, dim in enumerate(order):
             lines = math.prod(sizes[d] for d in order[k + 1:])
             shape = (lines, wide) if lines > 1 else (2, wide // 2)
@@ -467,20 +571,21 @@
         ((1, part_rows), i32),
         ((1, part_rows), i32),
         ((2, part_rows), i32),
-        ((CHUNKS, part_rows, wide), bf16),
         ((part_rows, padded), bf16),
         ((classes, 2, coef), bf16),
-        ((CHUNKS, half, wide), f32),
-        ((CHUNKS, half, wide), bf16),
-        ((CHUNKS, half, wide), bf16),
+        ((3, classes, padded), bf16),
         ((4, 1, width), f32),
         ((gx + gy + gz - 2, 1, width), f32),
         *hops, *hops,
+        *[((part_rows, 3 * span), bf16) for span in spans],
+        *[((half, 3 * span), f32) for span in spans],
+        *[((half, 3 * span), bf16) for span in spans],
+        *[((half, 3 * span), bf16) for span in spans],
     ]
     held = sum(math.prod(shape) * jnp.dtype(kind).itemsize for shape, kind in buffers)
     limit = min(60, held // 2**20 + 8) * 2**20
     scores, means, load = pl.pallas_call(
-        functools.partial(kernel, gx, gy, gz, span, coef, total),
+        functools.partial(kernel, gx, gy, gz, spans, coef, total),
         out_shape=(
             jax.ShapeDtypeStruct((part_rows, classes), f32),
             jax.ShapeDtypeStruct((1, 2, coef), f32),
@@ -489,7 +594,7 @@
         in_specs=[hbm] * 5,
         out_specs=(vmem, vmem, vmem),
         scratch_shapes=[pltpu.VMEM(shape, kind) for shape, kind in buffers] + [
-            dma((4 + PAIRS,)), dma((10,)), dma((CHUNKS,)), dma((3 * CHUNKS,)), dma((4,)), dma((4,)),
+            dma((4 + CHUNKS,)), dma((3 + 4 * (PIECES + 1) + 2,)), dma((CHUNKS,)), dma((3 * CHUNKS,)), dma((4,)), dma((4,)),
         ],
         compiler_params=pltpu.CompilerParams(
             collective_id=0, has_side_effects=True, vmem_limit_bytes=limit

time: 23.4 us -> 22.5 us (0.962)
  the two profiles are of different devices: /device:TPU:1 before, /device:TPU:0 now
where the time goes in v3:
time: 22.5 us; the launch traced here: 22.4 us
  Pallas kernels  21.8 us (97%)
  between operations  0.64 us (3%)
    pallas_call x1, Pallas kernels, body(): pl.pallas_call(functools.partial(kernel, gx, gy, gz, spans, coef, total),...  21.1 us
    pallas_call x1, Pallas kernels, finish(): pl.pallas_call(put, out_shape=tuple((jax.ShapeDtypeStruct(a.shape, a.dtyp...  0.66 us

profile of v3, /device:TPU:0, one launch (start us, length us, event | category | flops | bytes accessed | tf_op | source)
XLA Modules:
  0.0 22.4 jit_solution(10652191122915880421)
XLA Ops:
  0.6 21.1 %shard_map.76 = (f32[32,32]{1,0:T(8,128)S(1)}, f32[1,2,7488]{2,1,0:T(2,128)S(1)}, f32[1,32]{1,0:T(1,128)S(1)}) custom-call(bf16[32,2,7488]{2,1,0:T(2,128)(2,1)} %part_hbm.1, bf16[1,2,7488]{2,1,0:T(2,128)(2,1)} %ref_hbm.1, s32[1,32]{1,0:T(1,128)} %bitcast.3, s32[1,32]{1,0:T(1,128)} %bitcast.4, s32[2,32]{1,0:T(2,128)} %tilt_hbm.1), custom_call_target="tpu_custom_call" | custom-call | tf_op jit(solution)/shard_map/pallas_call | solution.py:587
  21.7 0.7 %shard_map.77 = (f32[32,32]{1,0:T(8,128)}, f32[1,2,7488]{2,1,0:T(2,128)}, f32[1,32]{1,0:T(1,128)}) custom-call(f32[32,32]{1,0:T(8,128)S(1)} %get-tuple-element.9.refs_0_, f32[1,2,7488]{2,1,0:T(2,128)S(1)} %get-tuple-element.10.refs_1_, f32[1,32]{1,0:T(1,128)S(1)} %get-tuple-element.11.refs_2_), custom_call_target="tpu_custom_call" | custom-call | tf_op jit(solution)/shard_map/pallas_call | solution.py:532

commit v4 on v3

--- a/solution.py
+++ b/solution.py
@@ -16,7 +16,7 @@
 LANES = 128
 MESH = pl.DeviceIdType.MESH
 
-SHARES = (10, 10, 10, 10, 10, 10)
+SHARES = (14, 14, 8, 8, 8, 8)
 CHUNKS = len(SHARES)
 SUB = 640
 ORDERS = ("xzy", "yzx", "xyz", "yxz", "xyz", "yxz")
@@ -96,11 +96,15 @@
     def y_cross(j):
         return device(x, lax.rem(y + j, gy), z, 1 - core)
 
+    def z_cross(j):
+        return device(x, y, lax.rem(z + j, gz), 1 - core)
+
     def z_peer(j):
         return device(x, y, lax.rem(z + j, gz), core)
 
     sizes = {"x": gx, "y": gy, "z": gz}
     peer_of = {"x": x_peer, "y": y_peer, "z": z_peer}
+    cross_of = {"x": x_cross, "y": y_cross, "z": z_cross}
 
     def fetch(src, dst, at):
         copy = pltpu.make_async_copy(src, dst, in_sems.at[at])
@@ -114,6 +118,7 @@
     peers += [z_peer(j) for j in range(1, gz)]
     peers += [x_cross(j) for j in range(1, gx)]
     peers += [y_cross(j) for j in range(1, gy)]
+    peers += [z_cross(j) for j in range(1, gz)]
     for peer in peers:
         pl.semaphore_signal(barrier, inc=1, device_id=(peer,), device_id_type=MESH)
     metas = [
@@ -167,9 +172,9 @@
         if at == end:
             return
         for j in range(1, gx):
-            give(at, slot(gx - j, 0, 0) + at, end - at, every, sem, x_peer(j))
+            give(at, slot(gx - j, 0, 1) + at, end - at, every, sem, x_cross(j))
         for j in range(1, gy):
-            give(at, slot(0, gy - j, 0) + at, end - at, every, sem + 1, y_peer(j))
+            give(at, slot(0, gy - j, 1) + at, end - at, every, sem + 1, y_cross(j))
         give(at, slot(0, 0, 1) + at, end - at, every, 0, sibling)
 
     def ag_forward(g):
@@ -181,20 +186,20 @@
             arrived(all_ref.at[pl.ds(0, (gx - 1) * n)], ag_sems.at[sem])
         for dx in range(1, gx):
             for j in range(1, gy):
-                give(slot(dx, 0, 0) + at, slot(dx, gy - j, 0) + at, n, front, sem + 2, y_peer(j))
+                give(slot(dx, 0, 1) + at, slot(dx, gy - j, 1) + at, n, front, sem + 2, y_peer(j))
                 if g == PIECES - 1:
-                    give(slot(dx, 0, 0) + at, slot(dx, gy - j, 1) + at, n, front, cross, y_cross(j))
+                    give(slot(dx, 0, 1) + at, slot(dx, gy - j, 0) + at, n, front, cross, y_cross(j))
         if gy > 1:
             arrived(all_ref.at[pl.ds(0, (gy - 1) * n)], ag_sems.at[sem + 1])
         for dy in range(1, gy):
             for j in range(1, gx):
-                give(slot(0, dy, 0) + at, slot(gx - j, dy, 0) + at, n, back, sem + 3, x_peer(j))
+                give(slot(0, dy, 1) + at, slot(gx - j, dy, 1) + at, n, back, sem + 3, x_peer(j))
                 if g == PIECES - 1:
-                    give(slot(0, dy, 0) + at, slot(gx - j, dy, 1) + at, n, back, cross + 1, x_cross(j))
+                    give(slot(0, dy, 1) + at, slot(gx - j, dy, 0) + at, n, back, cross + 1, x_cross(j))
         for dx in range(1, gx):
-            give(slot(dx, 0, 0) + at, slot(dx, 0, 1) + at, n, every, 0, sibling)
+            give(slot(dx, 0, 1) + at, slot(dx, 0, 0) + at, n, every, 0, sibling)
         for dy in range(1, gy):
-            give(slot(0, dy, 0) + at, slot(0, dy, 1) + at, n, every, 0, sibling)
+            give(slot(0, dy, 1) + at, slot(0, dy, 0) + at, n, every, 0, sibling)
 
     def ag_core(g):
         at, end = split(g) if g >= 0 else (0, 1)
@@ -207,7 +212,7 @@
             return
         for dx in range(1, gx):
             for dy in range(1, gy):
-                give(slot(dx, dy, 0) + at, slot(dx, dy, 1) + at, n, every, 1, sibling)
+                give(slot(dx, dy, 1) + at, slot(dx, dy, 0) + at, n, every, 1, sibling)
 
     def ag_own():
         own_ref.wait()
@@ -249,18 +254,18 @@
 
     row = lax.broadcasted_iota(jnp.int32, (classes, 1), 0)
 
-    def ids_of(order):
+    def ids_of(order, flip):
         left, at = row, {}
         for dim in reversed(order):
             at[dim] = left & (sizes[dim] - 1)
             left = lax.shift_right_logical(left, log2(sizes[dim]))
-        return device((at["x"] + x) & (gx - 1), (at["y"] + y) & (gy - 1), (at["z"] + z) & (gz - 1), (left + core) & 1)
-
-    ids = ids_of("xyz")
+        return device((at["x"] + x) & (gx - 1), (at["y"] + y) & (gy - 1), (at["z"] + z) & (gz - 1), (left + core + flip) & 1)
+
+    ids = ids_of("xyz", 0)
     onehot = {}
     for order in ORDERS:
         if order not in onehot:
-            onehot[order] = jnp.where(ids_of(order).astype(jnp.float32) == cls_row, 1.0, 0.0).astype(jnp.bfloat16)
+            onehot[order] = jnp.where(ids_of(order, 1).astype(jnp.float32) == cls_row, 1.0, 0.0).astype(jnp.bfloat16)
     sums = {"wedge": jnp.zeros((rows, 1), jnp.float32), "power": jnp.zeros((rows, 1), jnp.float32)}
 
     def parts(first, size):
@@ -318,12 +323,17 @@
             return mine[t][...] + recv_core[t][...].astype(jnp.float32)
         n = sizes[ORDERS[t][k]]
         lines = math.prod(sizes[dim] for dim in ORDERS[t][k + 1:])
+        recv = hop_recvs[3 * t + k]
+        if k == 1 or n > 1:
+            arrived(recv, hop_sems.at[3 * t + k])
+        if k == 1:
+            piece = recv[0].astype(jnp.float32)
+            for j in range(1, n):
+                piece = piece + recv[j].astype(jnp.float32)
+            return piece
         piece = mine[t][:lines]
         if lines == 1:
             piece = fold(piece)
-        recv = hop_recvs[3 * t + k]
-        if n > 1:
-            arrived(recv, hop_sems.at[3 * t + k])
         for j in range(1, n):
             piece = piece + recv[j - 1].astype(jnp.float32)
         return piece
@@ -333,13 +343,17 @@
         lines = math.prod(sizes[dim] for dim in ORDERS[t][k + 1:])
         piece = taken(t, k - 1)
         send, recv = hop_sends[3 * t + k], hop_recvs[3 * t + k]
-        for j in range(1, sizes[dim]):
+        for j in range(0 if k == 1 else 1, sizes[dim]):
             part_of = piece[j * lines:(j + 1) * lines]
             if lines == 1:
                 part_of = fold(part_of)
-            send[j - 1] = part_of.astype(jnp.bfloat16)
-            push(send.at[j - 1], recv.at[j - 1], send_sems.at[2], hop_sems.at[3 * t + k], peer_of[dim](j))
-        mine[t][:lines] = piece[:lines]
+            at = j if k == 1 else j - 1
+            send[at] = part_of.astype(jnp.bfloat16)
+            peer = sibling if j == 0 else (cross_of if k == 1 else peer_of)[dim](j)
+            sem = 4 + t if j == 0 else 2
+            push(send.at[at], recv.at[at], send_sems.at[sem], hop_sems.at[3 * t + k], peer)
+        if k != 1:
+            mine[t][:lines] = piece[:lines]
 
     def first(t):
         hop(t, 0)
@@ -351,7 +365,7 @@
         hop(t, 2)
 
     reach = small_send.shape[2] // 2
-    stages = [(1, lambda j: sibling)] + [(sizes[dim] - 1, peer_of[dim]) for dim in SMALL]
+    stages = [(1, lambda j: sibling)] + [(sizes[dim] - 1, (peer_of, cross_of, peer_of)[k][dim]) for k, dim in enumerate(SMALL)]
 
     def small_start():
         lane = lax.broadcasted_iota(jnp.int32, (rows, reach), 1).astype(jnp.float32)
@@ -420,10 +434,23 @@
             place = jnp.where(order[lines] == lane, 1.0, 0.0)
             table.append(jnp.dot(value, place, precision=lax.Precision.HIGHEST, preferred_element_type=jnp.float32))
 
-    def score_early():
-        prepare([(begin, end) for begin, end in early if end <= half])
+    groups = [(at, at + gz) for begin, end in early for at in range(begin, end, gz)]
+
+    def merged(runs):
+        out = []
+        for begin, end in runs:
+            if out and out[-1][1] == begin and begin != half:
+                out[-1] = (out[-1][0], end)
+            else:
+                out.append((begin, end))
+        return out
+
+    def prepare_near():
+        prepare(merged([g for g in groups if (g[0] < half) == (g[0] % half == 0)]))
+
+    def prepare_far():
         arrived(all_ref.at[pl.ds(0, half - diag)], ag_sems.at[0])
-        prepare([(begin, end) for begin, end in early if end > half])
+        prepare(merged([g for g in groups if (g[0] < half) != (g[0] % half == 0)]))
 
     def score_late():
         last = (gx - 1) * (gy - 1) * (gz - split(PIECES - 1)[0])
@@ -482,15 +509,13 @@
     ag_direct(0)
     ag_direct(1)
     ag_direct(2)
-    ag_core(-1)
     hop(2, 1)
     hop(3, 1)
+    ag_core(-1)
     small_next(1)
     hop(4, 1)
     hop(5, 1)
     ag_forward(0)
-    hop(0, 2)
-    hop(1, 2)
     ag_forward(1)
     ag_forward(2)
     small_next(2)
@@ -498,9 +523,12 @@
     hop(3, 2)
     hop(4, 2)
     hop(5, 2)
-    score_early()
+    hop(0, 2)
+    hop(1, 2)
+    prepare_near()
     ag_core(0)
     ag_core(1)
+    prepare_far()
     score(0, classes - 2 * diag)
     ag_core(2)
     score_late()
@@ -516,6 +544,8 @@
     whole_of(ready.at[:, :half, :], send_sems.at[1]).wait_send()
     whole_of(all_ref.at[pl.ds(0, classes - 2), :, :3 * sum(spans) // 4], send_sems.at[2]).wait_send()
     whole_of(small_recv, send_sems.at[3]).wait_send()
+    for t in range(CHUNKS):
+        whole_of(hop_sends[3 * t + 1].at[0], send_sems.at[4 + t]).wait_send()
 
 
 def finish(*arrays):
@@ -565,7 +595,7 @@
         for k, dim in enumerate(order):
             lines = math.prod(sizes[d] for d in order[k + 1:])
             shape = (lines, wide) if lines > 1 else (2, wide // 2)
-            hops.append(((max(1, sizes[dim] - 1), *shape), bf16))
+            hops.append(((max(1, sizes[dim] - (k != 1)), *shape), bf16))
     buffers = [
         ((part_rows, 2, coef), bf16),
         ((1, part_rows), i32),
@@ -594,7 +624,7 @@
         in_specs=[hbm] * 5,
         out_specs=(vmem, vmem, vmem),
         scratch_shapes=[pltpu.VMEM(shape, kind) for shape, kind in buffers] + [
-            dma((4 + CHUNKS,)), dma((3 + 4 * (PIECES + 1) + 2,)), dma((CHUNKS,)), dma((3 * CHUNKS,)), dma((4,)), dma((4,)),
+            dma((4 + CHUNKS,)), dma((3 + 4 * (PIECES + 1) + 2,)), dma((CHUNKS,)), dma((3 * CHUNKS,)), dma((4,)), dma((4 + CHUNKS,)),
         ],
         compiler_params=pltpu.CompilerParams(
             collective_id=0, has_side_effects=True, vmem_limit_bytes=limit

time: 22.5 us -> 22.2 us (0.987)
  Pallas kernels: 21.8 us -> 21.4 us
    pallas_call x1, Pallas kernels: 21.1 us -> 20.8 us  [body(): pl.pallas_call(functools.partial(kernel, gx, gy, gz, spans, coef, total),...]
where the time goes in v4:
time: 22.2 us; the launch traced here: 22.1 us
  Pallas kernels  21.4 us (96%)
  between operations  0.64 us (3%)
    pallas_call x1, Pallas kernels, body(): pl.pallas_call(functools.partial(kernel, gx, gy, gz, spans, coef, total),...  20.8 us
    pallas_call x1, Pallas kernels, finish(): pl.pallas_call(put, out_shape=tuple((jax.ShapeDtypeStruct(a.shape, a.dtyp...  0.66 us

profile of v4, /device:TPU:0, one launch (start us, length us, event | category | flops | bytes accessed | tf_op | source)
XLA Modules:
  0.0 22.1 jit_solution(11849017914606957625)
XLA Ops:
  0.6 20.8 %shard_map.76 = (f32[32,32]{1,0:T(8,128)S(1)}, f32[1,2,7488]{2,1,0:T(2,128)S(1)}, f32[1,32]{1,0:T(1,128)S(1)}) custom-call(bf16[32,2,7488]{2,1,0:T(2,128)(2,1)} %part_hbm.1, bf16[1,2,7488]{2,1,0:T(2,128)(2,1)} %ref_hbm.1, s32[1,32]{1,0:T(1,128)} %bitcast.3, s32[1,32]{1,0:T(1,128)} %bitcast.4, s32[2,32]{1,0:T(2,128)} %tilt_hbm.1), custom_call_target="tpu_custom_call" | custom-call | tf_op jit(solution)/shard_map/pallas_call | solution.py:617
  21.4 0.7 %shard_map.77 = (f32[32,32]{1,0:T(8,128)}, f32[1,2,7488]{2,1,0:T(2,128)}, f32[1,32]{1,0:T(1,128)}) custom-call(f32[32,32]{1,0:T(8,128)S(1)} %get-tuple-element.9.refs_0_, f32[1,2,7488]{2,1,0:T(2,128)S(1)} %get-tuple-element.10.refs_1_, f32[1,32]{1,0:T(1,128)S(1)} %get-tuple-element.11.refs_2_), custom_call_target="tpu_custom_call" | custom-call | tf_op jit(solution)/shard_map/pallas_call | solution.py:562

commit v5 on v4

--- a/solution.py
+++ b/solution.py
@@ -66,7 +66,10 @@
 ):
     hop_sends, hop_recvs = rest[:3 * CHUNKS], rest[3 * CHUNKS:6 * CHUNKS]
     data, mine, send_core, recv_core = (rest[k * CHUNKS:(k + 1) * CHUNKS] for k in range(6, 10))
-    in_sems, ag_sems, core_sems, hop_sems, small_sems, send_sems = rest[10 * CHUNKS:]
+    extra = CHUNKS // 2
+    core_pairs = recv_core[:CHUNKS // 2]
+    recv_core = [core_pairs[t // 2].at[t % 2] for t in range(CHUNKS)]
+    in_sems, ag_sems, core_sems, hop_sems, small_sems, send_sems = rest[10 * CHUNKS - extra:]
     starts = [sum(spans[:t]) for t in range(CHUNKS)]
     widths = [max(0, min(spans[t], coef - starts[t])) for t in range(CHUNKS)]
     me = lax.axis_index("dom")
@@ -128,9 +131,9 @@
     ]
     own_ref = fetch(ref_hbm.at[0], all_ref.at[0], 0)
     part_copies = []
-    for t in range(CHUNKS):
-        cols = pl.ds(starts[t], widths[t])
-        part_copies.append(fetch(part_hbm.at[:, :, cols], part.at[:, :, cols], 4 + t))
+    for t in range(0, CHUNKS, 2):
+        cols = pl.ds(starts[t], widths[t] + widths[t + 1])
+        part_copies.append(fetch(part_hbm.at[:, :, cols], part.at[:, :, cols], 4 + t // 2))
 
     def push(src, dst, send_sem, recv_sem, target):
         pltpu.make_async_remote_copy(
@@ -162,7 +165,7 @@
         return 1 + g * (gz - 1) // PIECES, 1 + (g + 1) * (gz - 1) // PIECES
 
     def sem_of(g):
-        return 3 + 4 * (g + 1)
+        return 3 + 2 * (g + 1)
 
     cross = sem_of(PIECES)
 
@@ -174,7 +177,7 @@
         for j in range(1, gx):
             give(at, slot(gx - j, 0, 1) + at, end - at, every, sem, x_cross(j))
         for j in range(1, gy):
-            give(at, slot(0, gy - j, 1) + at, end - at, every, sem + 1, y_cross(j))
+            give(at, slot(0, gy - j, 1) + at, end - at, every, sem, y_cross(j))
         give(at, slot(0, 0, 1) + at, end - at, every, 0, sibling)
 
     def ag_forward(g):
@@ -182,20 +185,18 @@
         n, sem = end - at, sem_of(g)
         if n == 0:
             return
-        if gx > 1:
-            arrived(all_ref.at[pl.ds(0, (gx - 1) * n)], ag_sems.at[sem])
+        if gx + gy > 2:
+            arrived(all_ref.at[pl.ds(0, (gx + gy - 2) * n)], ag_sems.at[sem])
         for dx in range(1, gx):
             for j in range(1, gy):
-                give(slot(dx, 0, 1) + at, slot(dx, gy - j, 1) + at, n, front, sem + 2, y_peer(j))
+                give(slot(dx, 0, 1) + at, slot(dx, gy - j, 1) + at, n, front, sem + 1, y_peer(j))
                 if g == PIECES - 1:
                     give(slot(dx, 0, 1) + at, slot(dx, gy - j, 0) + at, n, front, cross, y_cross(j))
-        if gy > 1:
-            arrived(all_ref.at[pl.ds(0, (gy - 1) * n)], ag_sems.at[sem + 1])
         for dy in range(1, gy):
             for j in range(1, gx):
-                give(slot(0, dy, 1) + at, slot(gx - j, dy, 1) + at, n, back, sem + 3, x_peer(j))
+                give(slot(0, dy, 1) + at, slot(gx - j, dy, 1) + at, n, back, sem + 1, x_peer(j))
                 if g == PIECES - 1:
-                    give(slot(0, dy, 1) + at, slot(gx - j, dy, 0) + at, n, back, cross + 1, x_cross(j))
+                    give(slot(0, dy, 1) + at, slot(gx - j, dy, 0) + at, n, back, cross, x_cross(j))
         for dx in range(1, gx):
             give(slot(dx, 0, 1) + at, slot(dx, 0, 0) + at, n, every, 0, sibling)
         for dy in range(1, gy):
@@ -206,8 +207,7 @@
         n, sem = end - at, sem_of(g)
         count = (gx - 1) * (gy - 1) * n
         if count:
-            arrived(all_ref.at[pl.ds(0, count), :, front], ag_sems.at[sem + 2])
-            arrived(all_ref.at[pl.ds(0, count), :, back], ag_sems.at[sem + 3])
+            arrived(all_ref.at[pl.ds(0, count)], ag_sems.at[sem + 1])
         if g == PIECES - 1:
             return
         for dx in range(1, gx):
@@ -293,7 +293,8 @@
 
     def compute(t):
         span = spans[t]
-        part_copies[t].wait()
+        if t % 2 == 0:
+            part_copies[t // 2].wait()
         for at in range(0, span, SUB):
             first = starts[t] + at
             size = min(SUB, span - at)
@@ -311,7 +312,7 @@
             mine[t][:, cols] = both[:half]
 
     def cores(t):
-        push(send_core[t], recv_core[t], send_sems.at[1], core_sems.at[t], sibling)
+        push(send_core[t], recv_core[t], send_sems.at[1], core_sems.at[t // 2], sibling)
 
     def fold(line):
         wide = line.shape[1]
@@ -319,7 +320,8 @@
 
     def taken(t, k):
         if k < 0:
-            arrived(recv_core[t], core_sems.at[t])
+            if t % 2 == 0:
+                arrived(core_pairs[t // 2], core_sems.at[t // 2])
             return mine[t][...] + recv_core[t][...].astype(jnp.float32)
         n = sizes[ORDERS[t][k]]
         lines = math.prod(sizes[dim] for dim in ORDERS[t][k + 1:])
@@ -350,7 +352,7 @@
             at = j if k == 1 else j - 1
             send[at] = part_of.astype(jnp.bfloat16)
             peer = sibling if j == 0 else (cross_of if k == 1 else peer_of)[dim](j)
-            sem = 4 + t if j == 0 else 2
+            sem = 4 if j == 0 else 2
             push(send.at[at], recv.at[at], send_sems.at[sem], hop_sems.at[3 * t + k], peer)
         if k != 1:
             mine[t][:lines] = piece[:lines]
@@ -457,8 +459,7 @@
         if diag > last:
             arrived(all_ref.at[pl.ds(0, diag - last)], ag_sems.at[1])
         if last:
-            arrived(all_ref.at[pl.ds(0, last), :, front], ag_sems.at[cross])
-            arrived(all_ref.at[pl.ds(0, last), :, back], ag_sems.at[cross + 1])
+            arrived(all_ref.at[pl.ds(0, last)], ag_sems.at[cross])
         prepare(late)
         score(classes - 2 * diag, classes)
         scores_ref[...] = sum(table[1:], table[0])
@@ -499,10 +500,10 @@
     small_start()
     hop(2, 0)
     hop(3, 0)
-    ag_forward(-1)
     small_next(0)
     hop(4, 0)
     hop(5, 0)
+    ag_forward(-1)
     hop(0, 1)
     hop(1, 1)
     ag_z()
@@ -511,10 +512,10 @@
     ag_direct(2)
     hop(2, 1)
     hop(3, 1)
-    ag_core(-1)
     small_next(1)
     hop(4, 1)
     hop(5, 1)
+    ag_core(-1)
     ag_forward(0)
     ag_forward(1)
     ag_forward(2)
@@ -544,8 +545,9 @@
     whole_of(ready.at[:, :half, :], send_sems.at[1]).wait_send()
     whole_of(all_ref.at[pl.ds(0, classes - 2), :, :3 * sum(spans) // 4], send_sems.at[2]).wait_send()
     whole_of(small_recv, send_sems.at[3]).wait_send()
-    for t in range(CHUNKS):
-        whole_of(hop_sends[3 * t + 1].at[0], send_sems.at[4 + t]).wait_send()
+    kept = sum(3 * spans[t] * sizes[ORDERS[t][2]] for t in range(CHUNKS)) // (2 * LANES)
+    lines = next(n for n in range(classes, 0, -1) if kept % n == 0 and kept // n * LANES <= coef)
+    whole_of(all_ref.at[pl.ds(0, lines), :, :kept // lines * LANES], send_sems.at[4]).wait_send()
 
 
 def finish(*arrays):
@@ -610,7 +612,7 @@
         *[((part_rows, 3 * span), bf16) for span in spans],
         *[((half, 3 * span), f32) for span in spans],
         *[((half, 3 * span), bf16) for span in spans],
-        *[((half, 3 * span), bf16) for span in spans],
+        *[((2, half, 3 * span), bf16) for span in spans[::2]],
     ]
     held = sum(math.prod(shape) * jnp.dtype(kind).itemsize for shape, kind in buffers)
     limit = min(60, held // 2**20 + 8) * 2**20
@@ -624,7 +626,7 @@
         in_specs=[hbm] * 5,
         out_specs=(vmem, vmem, vmem),
         scratch_shapes=[pltpu.VMEM(shape, kind) for shape, kind in buffers] + [
-            dma((4 + CHUNKS,)), dma((3 + 4 * (PIECES + 1) + 2,)), dma((CHUNKS,)), dma((3 * CHUNKS,)), dma((4,)), dma((4 + CHUNKS,)),
+            dma((4 + CHUNKS // 2,)), dma((3 + 2 * (PIECES + 1) + 1,)), dma((CHUNKS // 2,)), dma((3 * CHUNKS,)), dma((4,)), dma((5,)),
         ],
         compiler_params=pltpu.CompilerParams(
             collective_id=0, has_side_effects=True, vmem_limit_bytes=limit

time: 22.2 us -> 22.1 us (level)
  no operation moved by 1% of the time
where the time goes in v5:
time: 22.1 us; the launch traced here: 21.9 us
  Pallas kernels  21.3 us (96%)
  between operations  0.64 us (3%)
    pallas_call x1, Pallas kernels, body(): pl.pallas_call(functools.partial(kernel, gx, gy, gz, spans, coef, total),...  20.6 us
    pallas_call x1, Pallas kernels, finish(): pl.pallas_call(put, out_shape=tuple((jax.ShapeDtypeStruct(a.shape, a.dtyp...  0.66 us

profile of v5, /device:TPU:0, one launch (start us, length us, event | category | flops | bytes accessed | tf_op | source)
XLA Modules:
  0.0 21.9 jit_solution(16053773904233514472)
XLA Ops:
  0.6 20.6 %shard_map.76 = (f32[32,32]{1,0:T(8,128)S(1)}, f32[1,2,7488]{2,1,0:T(2,128)S(1)}, f32[1,32]{1,0:T(1,128)S(1)}) custom-call(bf16[32,2,7488]{2,1,0:T(2,128)(2,1)} %part_hbm.1, bf16[1,2,7488]{2,1,0:T(2,128)(2,1)} %ref_hbm.1, s32[1,32]{1,0:T(1,128)} %bitcast.3, s32[1,32]{1,0:T(1,128)} %bitcast.4, s32[2,32]{1,0:T(2,128)} %tilt_hbm.1), custom_call_target="tpu_custom_call" | custom-call | tf_op jit(solution)/shard_map/pallas_call | solution.py:619
  21.3 0.7 %shard_map.77 = (f32[32,32]{1,0:T(8,128)}, f32[1,2,7488]{2,1,0:T(2,128)}, f32[1,32]{1,0:T(1,128)}) custom-call(f32[32,32]{1,0:T(8,128)S(1)} %get-tuple-element.9.refs_0_, f32[1,2,7488]{2,1,0:T(2,128)S(1)} %get-tuple-element.10.refs_1_, f32[1,32]{1,0:T(1,128)S(1)} %get-tuple-element.11.refs_2_), custom_call_target="tpu_custom_call" | custom-call | tf_op jit(solution)/shard_map/pallas_call | solution.py:564

commit v6 on v5

--- a/solution.py
+++ b/solution.py
@@ -515,7 +515,6 @@
     small_next(1)
     hop(4, 1)
     hop(5, 1)
-    ag_core(-1)
     ag_forward(0)
     ag_forward(1)
     ag_forward(2)
@@ -524,13 +523,14 @@
     hop(3, 2)
     hop(4, 2)
     hop(5, 2)
+    ag_core(-1)
     hop(0, 2)
     hop(1, 2)
     prepare_near()
     ag_core(0)
-    ag_core(1)
     prepare_far()
     score(0, classes - 2 * diag)
+    ag_core(1)
     ag_core(2)
     score_late()
     counts()

time: 22.1 us -> 22.1 us (level)
  no operation moved by 1% of the time
where the time goes in v6:
time: 22.1 us; the launch traced here: 21.9 us
  Pallas kernels  21.3 us (96%)
  between operations  0.64 us (3%)
    pallas_call x1, Pallas kernels, body(): pl.pallas_call(functools.partial(kernel, gx, gy, gz, spans, coef, total),...  20.6 us
    pallas_call x1, Pallas kernels, finish(): pl.pallas_call(put, out_shape=tuple((jax.ShapeDtypeStruct(a.shape, a.dtyp...  0.66 us

profile of v6, /device:TPU:0, one launch (start us, length us, event | category | flops | bytes accessed | tf_op | source)
XLA Modules:
  0.0 21.9 jit_solution(1116964367857019571)
XLA Ops:
  0.6 20.6 %shard_map.76 = (f32[32,32]{1,0:T(8,128)S(1)}, f32[1,2,7488]{2,1,0:T(2,128)S(1)}, f32[1,32]{1,0:T(1,128)S(1)}) custom-call(bf16[32,2,7488]{2,1,0:T(2,128)(2,1)} %part_hbm.1, bf16[1,2,7488]{2,1,0:T(2,128)(2,1)} %ref_hbm.1, s32[1,32]{1,0:T(1,128)} %bitcast.3, s32[1,32]{1,0:T(1,128)} %bitcast.4, s32[2,32]{1,0:T(2,128)} %tilt_hbm.1), custom_call_target="tpu_custom_call" | custom-call | tf_op jit(solution)/shard_map/pallas_call | solution.py:619
  21.3 0.7 %shard_map.77 = (f32[32,32]{1,0:T(8,128)}, f32[1,2,7488]{2,1,0:T(2,128)}, f32[1,32]{1,0:T(1,128)}) custom-call(f32[32,32]{1,0:T(8,128)S(1)} %get-tuple-element.9.refs_0_, f32[1,2,7488]{2,1,0:T(2,128)S(1)} %get-tuple-element.10.refs_1_, f32[1,32]{1,0:T(1,128)S(1)} %get-tuple-element.11.refs_2_), custom_call_target="tpu_custom_call" | custom-call | tf_op jit(solution)/shard_map/pallas_call | solution.py:564

commit v7 on v6

--- a/solution.py
+++ b/solution.py
@@ -114,6 +114,17 @@
         copy.start()
         return copy
 
+    metas = [
+        fetch(orient_hbm, orient_ref, 1),
+        fetch(tilt_hbm, tilt_ref, 2),
+        fetch(cls_hbm, cls_ref, 3),
+    ]
+    own_ref = fetch(ref_hbm.at[0], all_ref.at[0], 0)
+    part_copies = []
+    for t in range(0, CHUNKS, 2):
+        cols = pl.ds(starts[t], widths[t] + widths[t + 1])
+        part_copies.append(fetch(part_hbm.at[:, :, cols], part.at[:, :, cols], 4 + t // 2))
+
     barrier = pltpu.get_barrier_semaphore()
     peers = [sibling]
     peers += [x_peer(j) for j in range(1, gx)]
@@ -124,16 +135,6 @@
     peers += [z_cross(j) for j in range(1, gz)]
     for peer in peers:
         pl.semaphore_signal(barrier, inc=1, device_id=(peer,), device_id_type=MESH)
-    metas = [
-        fetch(orient_hbm, orient_ref, 1),
-        fetch(tilt_hbm, tilt_ref, 2),
-        fetch(cls_hbm, cls_ref, 3),
-    ]
-    own_ref = fetch(ref_hbm.at[0], all_ref.at[0], 0)
-    part_copies = []
-    for t in range(0, CHUNKS, 2):
-        cols = pl.ds(starts[t], widths[t] + widths[t + 1])
-        part_copies.append(fetch(part_hbm.at[:, :, cols], part.at[:, :, cols], 4 + t // 2))
 
     def push(src, dst, send_sem, recv_sem, target):
         pltpu.make_async_remote_copy(
@@ -518,9 +519,9 @@
     ag_forward(0)
     ag_forward(1)
     ag_forward(2)
-    small_next(2)
     hop(2, 2)
     hop(3, 2)
+    small_next(2)
     hop(4, 2)
     hop(5, 2)
     ag_core(-1)

time: 22.1 us -> 22.1 us (level)
  no operation moved by 1% of the time
where the time goes in v7:
time: 22.1 us; the launch traced here: 21.9 us
  Pallas kernels  21.3 us (96%)
  between operations  0.64 us (3%)
    pallas_call x1, Pallas kernels, body(): pl.pallas_call(functools.partial(kernel, gx, gy, gz, spans, coef, total),...  20.6 us
    pallas_call x1, Pallas kernels, finish(): pl.pallas_call(put, out_shape=tuple((jax.ShapeDtypeStruct(a.shape, a.dtyp...  0.66 us

profile of v7, /device:TPU:0, one launch (start us, length us, event | category | flops | bytes accessed | tf_op | source)
XLA Modules:
  0.0 21.9 jit_solution(5647633000707959415)
XLA Ops:
  0.6 20.6 %shard_map.76 = (f32[32,32]{1,0:T(8,128)S(1)}, f32[1,2,7488]{2,1,0:T(2,128)S(1)}, f32[1,32]{1,0:T(1,128)S(1)}) custom-call(bf16[32,2,7488]{2,1,0:T(2,128)(2,1)} %part_hbm.1, bf16[1,2,7488]{2,1,0:T(2,128)(2,1)} %ref_hbm.1, s32[1,32]{1,0:T(1,128)} %bitcast.3, s32[1,32]{1,0:T(1,128)} %bitcast.4, s32[2,32]{1,0:T(2,128)} %tilt_hbm.1), custom_call_target="tpu_custom_call" | custom-call | tf_op jit(solution)/shard_map/pallas_call | solution.py:620
  21.3 0.7 %shard_map.77 = (f32[32,32]{1,0:T(8,128)}, f32[1,2,7488]{2,1,0:T(2,128)}, f32[1,32]{1,0:T(1,128)}) custom-call(f32[32,32]{1,0:T(8,128)S(1)} %get-tuple-element.9.refs_0_, f32[1,2,7488]{2,1,0:T(2,128)S(1)} %get-tuple-element.10.refs_1_, f32[1,32]{1,0:T(1,128)S(1)} %get-tuple-element.11.refs_2_), custom_call_target="tpu_custom_call" | custom-call | tf_op jit(solution)/shard_map/pallas_call | solution.py:565
